TPU v7x, 128 devices: a whole 4x4x4 slice. The times are simulated.
128 devices in a mesh: shard: 8 (over y, x_lo), cols: 16 (over z, x_hi, core).
Axes of the slice: x: 4 (x_hi: 2, x_lo: 2; x = x_hi * 2 + x_lo), y: 4, z: 4, core: 2. Of those that a mesh axis runs over, the one named last changes fastest.
Arguments:
- train_gate: bfloat16 [4096, 14336], P('shard', 'cols'), may hold values from -0.09375 to 0.09375
- low_gate: bfloat16 [4096, 32], P('shard'), may hold values from -0.09375 to 0.09375
- high_gate: bfloat16 [32, 14336], P(None, 'cols'), may hold values from -1 to 1
- train_up: bfloat16 [4096, 14336], P('shard', 'cols'), may hold values from -0.09375 to 0.09375
- low_up: bfloat16 [4096, 32], P('shard'), may hold values from -0.09375 to 0.09375
- high_up: bfloat16 [32, 14336], P(None, 'cols'), may hold values from -1 to 1
- norm_train: float32 [4096], P(('shard', 'cols')), may hold values from 0.25 to 1.75
- norm_step: float32 [4096], P(('shard', 'cols')), may hold values from -0.3 to 0.3
Outputs:
- ready_gate: bfloat16 [14336, 4096], P('cols')
- ready_up: bfloat16 [14336, 4096], P('cols')
- serve_norm: bfloat16 [4096], replicated
All inputs are finite; a program needn't handle non-finite values.
Results may differ from a plain program's by a relative error of at most 0.001.
Values may be sent and summed in bfloat16 or wider, within the bound.
A program may use at most 128 MiB of HBM per device.

v0:
```python
import jax
import jax.numpy as jnp
from jax import lax
from jax.sharding import Mesh
from jax.sharding import PartitionSpec as P

SHARD = ("shard_0", "shard_1")
SHARD_COLS = ("shard_0", "shard_1", "cols")


mix_rate = 1.0


def edges_of(length, count):
    unit = 8 if length >= 8 * count else 1
    return [length // unit * k // count * unit for k in range(1, count)]


def stacked_from(x, axes, sequence):
    blocks = x
    for k in sequence:
        blocks = lax.all_gather(blocks, axes[k])
    done = sequence[::-1]
    back = [done.index(k) for k in range(len(axes))]
    blocks = blocks.transpose(*back, *range(len(axes), blocks.ndim))
    return blocks.reshape(-1, *x.shape)


def in_order(blocks, dim):
    blocks = jnp.moveaxis(blocks, 0, dim)
    shape = blocks.shape
    return blocks.reshape(*shape[:dim], shape[dim] * shape[dim + 1], *shape[dim + 2 :])


def gather_all_axes(x, axes, dim):
    numbers = list(range(len(axes)))[::-1]
    widest = x.shape.index(max(x.shape[:-1] or x.shape))
    edges = [0, *edges_of(x.shape[widest], len(axes)), x.shape[widest]]
    gathered = []
    for k, (start, end) in enumerate(zip(edges, edges[1:])):
        if end > start:
            piece = lax.slice_in_dim(x, start, end, axis=widest)
            gathered.append(stacked_from(piece, axes, numbers[k:] + numbers[:k]))
    return in_order(jnp.concatenate(gathered, axis=widest + 1), dim)


def per_device(train_gate, low_gate, high_gate, train_up, low_up, high_up, norm_train, norm_step):
    latest_gate = train_gate.astype(jnp.float32) + mix_rate * jnp.dot(
        low_gate, high_gate, preferred_element_type=jnp.float32
    )
    latest_up = train_up.astype(jnp.float32) + mix_rate * jnp.dot(
        low_up, high_up, preferred_element_type=jnp.float32
    )
    narrow_gate, narrow_up = (latest_gate.astype(jnp.bfloat16), latest_up.astype(jnp.bfloat16))
    ready_gate, ready_up = (
        gather_all_axes(narrow_gate, SHARD, 0),
        gather_all_axes(narrow_up, SHARD, 0),
    )
    ready_gate, ready_up = (ready_gate.T, ready_up.T)
    serve_norm = lax.all_gather(
        (norm_train + norm_step).astype(jnp.bfloat16), SHARD_COLS, axis=0, tiled=True
    )
    return (ready_gate, ready_up, serve_norm)


def solution(mesh):
    finer = Mesh(mesh.devices.reshape(4, 2, mesh.shape["cols"]), ("shard_0", "shard_1", "cols"))
    placed = (
        P(SHARD, "cols"),
        P(SHARD, None),
        P(None, "cols"),
        P(SHARD, "cols"),
        P(SHARD, None),
        P(None, "cols"),
        P(SHARD_COLS),
        P(SHARD_COLS),
    )
    return jax.shard_map(
        per_device,
        mesh=finer,
        in_specs=placed,
        out_specs=(P("cols", None), P("cols", None), P()),
        check_vma=False,
    )
```

profile of v0, /device:TPU:0, one launch (start us, length us, event | category | flops | bytes accessed | tf_op | source)
XLA Modules:
  0.0 300.6 jit_solution(1203420934435352514)
XLA Ops:
  7.2 0.0 all-gather.23.cloned.1.call-start
  7.3 0.7 copy-done
  8.0 1.6 add_convert_fusion
  9.6 0.8 fusion
  10.5 0.0 all-gather.23.cloned.1.call-update
  10.5 0.0 all-gather.17.cloned.1.call-start
  10.6 0.4 add_convert_fusion.1
  11.0 0.8 fusion.1
  11.8 0.0 all-gather.17.cloned.1.call-update
  11.9 0.0 all-gather.25.cloned.1.call-start
  11.9 29.9 %all-gather.23.cloned.1.call-done = bf16[1024,896]{1,0:T(8,128)(2,1)} async-done(((bf16[256,896]{1,0:T(8,128)(2,1)}), bf16[1024,896]{1,0:T(8,128)(2,1)}) %all-gather.23.cloned.1.call-update) | async-done | bytes 1835024 | tf_op jit(solution)/shard_map/all_gather | solution.py:22
  41.8 0.0 all-gather.25.cloned.1.call-update
  41.8 0.0 all-gather.21.cloned.1.call-start
  41.9 12.9 %all-gather.4 = bf16[512,896]{1,0:T(8,128)(2,1)} all-gather(bf16[256,896]{1,0:T(8,128)(2,1)S(1)} %get-tuple-element.3), channel_id=6, replica_groups=mesh['shard_0'=4,'shard_1'=2,'cols'=16] {'shard_1'}, dimensions={0}, use_global_device_ids=true | all-gather | bytes 1376256 | tf_op jit(solution)/shard_map/all_gather | solution.py:22
  54.7 0.0 all-gather.21.cloned.1.call-update
  54.7 0.0 all-gather.19.cloned.1.call-start
  54.8 17.8 %all-gather.17.cloned.1.call-done = bf16[1024,896]{1,0:T(8,128)(2,1)} async-done(((bf16[256,896]{1,0:T(8,128)(2,1)}), bf16[1024,896]{1,0:T(8,128)(2,1)}) %all-gather.17.cloned.1.call-update) | async-done | bytes 1835024 | tf_op jit(solution)/shard_map/all_gather | solution.py:22
  72.6 0.0 all-gather.19.cloned.1.call-update
  72.6 0.0 all-gather.15.cloned.1.call-start
  72.7 12.9 %all-gather = bf16[512,896]{1,0:T(8,128)(2,1)} all-gather(bf16[256,896]{1,0:T(8,128)(2,1)S(1)} %get-tuple-element.5), channel_id=2, replica_groups=mesh['shard_0'=4,'shard_1'=2,'cols'=16] {'shard_1'}, dimensions={0}, use_global_device_ids=true | all-gather | bytes 1376256 | tf_op jit(solution)/shard_map/all_gather | solution.py:22
  85.5 0.0 all-gather.15.cloned.1.call-update
  85.6 0.2 dynamic-update-slice
  85.9 65.6 %all-reduce = bf16[4096]{0:T(1024)(128)(2,1)} all-reduce(bf16[4096]{0:T(1024)(128)(2,1)S(1)} %dynamic-update-slice), channel_id=1, replica_groups=mesh['shard_0'=4,'shard_1'=2,'cols'=16] {'shard_0','shard_1','cols'}, use_global_device_ids=true, to_apply=%add | all-reduce | flops 4096 | bytes 16384
  151.5 4.2 %copy.17 = bf16[2,4,256,896]{3,2,0,1:T(8,128)(2,1)} copy(bf16[2,4,256,896]{3,2,1,0:T(8,128)(2,1)} %bitcast.26) | data formatting | bytes 7340032 | tf_op jit(solution)/shard_map/all_gather | solution.py:22
  155.7 19.5 %all-gather.21.cloned.1.call-done = bf16[8,256,896]{2,1,0:T(8,128)(2,1)} async-done(((bf16[2,256,896]{2,1,0:T(8,128)(2,1)}), bf16[8,256,896]{2,1,0:T(8,128)(2,1)}) %all-gather.21.cloned.1.call-update) | async-done | bytes 3670032 | tf_op jit(solution)/shard_map/all_gather | solution.py:22
  175.2 6.8 %pad_maximum_fusion.1 = bf16[8,512,896]{2,1,0:T(8,128)(2,1)} fusion(bf16[8,256,896]{2,1,0:T(8,128)(2,1)} %bitcast.22, bf16[8,256,896]{2,1,0:T(8,128)(2,1)} %all-gather.21.cloned.1.call-done), kind=kLoop, calls=%fused_computation.1 | loop fusion | flops 14680064 | bytes 14680064 | tf_op jit(solution)/shard_map/concatenate | solution.py:44
  182.0 10.9 %copy.18 = bf16[4096,896]{0,1:T(8,128)(2,1)} copy(bf16[4096,896]{1,0:T(8,128)(2,1)} %bitcast.20) | data formatting | bytes 14680064 | tf_op jit(solution)/shard_map/reshape | solution.py:32
  192.9 37.0 %all-gather.19.cloned.1.call-done = bf16[8,256,896]{2,1,0:T(8,128)(2,1)} async-done(((bf16[4,256,896]{2,1,0:T(8,128)(2,1)}), bf16[8,256,896]{2,1,0:T(8,128)(2,1)}) %all-gather.19.cloned.1.call-update) | async-done | bytes 3670032 | tf_op jit(solution)/shard_map/all_gather | solution.py:22
  229.9 4.2 %copy.15 = bf16[2,4,256,896]{3,2,0,1:T(8,128)(2,1)} copy(bf16[2,4,256,896]{3,2,1,0:T(8,128)(2,1)} %bitcast.27) | data formatting | bytes 7340032 | tf_op jit(solution)/shard_map/all_gather | solution.py:22
  234.0 42.2 %all-gather.15.cloned.1.call-done = bf16[8,256,896]{2,1,0:T(8,128)(2,1)} async-done(((bf16[2,256,896]{2,1,0:T(8,128)(2,1)}), bf16[8,256,896]{2,1,0:T(8,128)(2,1)}) %all-gather.15.cloned.1.call-update) | async-done | bytes 3670032 | tf_op jit(solution)/shard_map/all_gather | solution.py:22
  276.3 6.7 %pad_maximum_fusion = bf16[8,512,896]{2,1,0:T(8,128)(2,1)} fusion(bf16[8,256,896]{2,1,0:T(8,128)(2,1)} %bitcast.23, bf16[8,256,896]{2,1,0:T(8,128)(2,1)} %all-gather.15.cloned.1.call-done), kind=kLoop, calls=%fused_computation | loop fusion | flops 14680064 | bytes 14680064 | tf_op jit(solution)/shard_map/concatenate | solution.py:44
  283.0 10.8 %copy.16 = bf16[4096,896]{0,1:T(8,128)(2,1)} copy(bf16[4096,896]{1,0:T(8,128)(2,1)} %bitcast.21) | data formatting | bytes 14680064 | tf_op jit(solution)/shard_map/reshape | solution.py:32
  (14 shorter events, 0.0 us)
Async XLA Ops:
  7.2 0.8 copy-start
  7.2 3.4 %copy-start.2 = (bf16[32,896]{1,0:T(8,128)(2,1)S(1)}, bf16[32,896]{1,0:T(8,128)(2,1)}, u32[]{:S(2)}) copy-start(bf16[32,896]{1,0:T(8,128)(2,1)} %param.10) | copy-start | bytes 172036
  7.2 3.4 %copy-start.1 = (bf16[512,896]{1,0:T(8,128)(2,1)S(1)}, bf16[512,896]{1,0:T(8,128)(2,1)}, u32[]{:S(2)}) copy-start(bf16[512,896]{1,0:T(8,128)(2,1)} %param.8) | copy-start | bytes 2752516
  7.2 3.4 %copy-start.3 = (bf16[512,32]{0,1:T(8,128)(2,1)S(1)}, bf16[512,32]{0,1:T(8,128)(2,1)}, u32[]{:S(2)}) copy-start(bf16[512,32]{0,1:T(8,128)(2,1)} %param.9) | copy-start | bytes 98308
  7.2 34.6 %all-gather.23.cloned.1.call-start = ((), (), s32[]{:S(2)}) async-start(), calls=%async_computation.4 | async-start | bytes 2293760 | tf_op jit(solution)/shard_map/all_gather | solution.py:22
  10.5 62.1 %all-gather.17.cloned.1.call-start = ((), (), s32[]{:S(2)}) async-start(), calls=%async_computation.1 | async-start | bytes 2293760 | tf_op jit(solution)/shard_map/all_gather | solution.py:22
  11.9 139.6 %all-gather.25.cloned.1.call-start = ((), (), s32[]{:S(2)}) async-start(), calls=%async_computation.5 | async-start | bytes 5505024 | tf_op jit(solution)/shard_map/all_gather | solution.py:22
  41.8 43.8 %copy-start.4 = (f32[32]{0:T(128)S(1)}, f32[32]{0:T(128)}, u32[]{:S(2)}) copy-start(f32[32]{0:T(128)} %param.14) | copy-start | bytes 388
  41.8 43.8 %copy-start.5 = (f32[32]{0:T(128)S(1)}, f32[32]{0:T(128)}, u32[]{:S(2)}) copy-start(f32[32]{0:T(128)} %param.15) | copy-start | bytes 388
  41.8 133.4 %all-gather.21.cloned.1.call-start = ((), (), s32[]{:S(2)}) async-start(), calls=%async_computation.3 | async-start | bytes 4587520 | tf_op jit(solution)/shard_map/all_gather | solution.py:22
  54.7 175.1 %all-gather.19.cloned.1.call-start = ((), (), s32[]{:S(2)}) async-start(), calls=%async_computation.2 | async-start | bytes 5505024 | tf_op jit(solution)/shard_map/all_gather | solution.py:22
  72.6 203.6 %all-gather.15.cloned.1.call-start = ((), (), s32[]{:S(2)}) async-start(), calls=%async_computation | async-start | bytes 4587520 | tf_op jit(solution)/shard_map/all_gather | solution.py:22
Sparse Core Ops, SparseCore 0:
  10.6 31.1 all-gather.22
  44.0 28.5 all-gather.16
  74.3 54.0 all-gather.24
  129.9 45.2 all-gather.20
  176.7 53.1 all-gather.18
  231.4 44.8 all-gather.14
where the time goes:
time: 302 us; the launch traced here: 301 us
  waiting for transfers between devices  146 us (48%)
  blocking collectives  91.4 us (30%)
  local copies, waits for them, and re-layouts  32.8 us (11%)
  between operations  14.2 us (5%)
  other arithmetic  13.5 us (4%)
    all_gather x6, waiting for transfers between devices, stacked_from(): blocks = lax.all_gather(blocks, axes[k])  146 us
    unnamed x1, blocking collectives  65.6 us
    all_gather x2, blocking collectives, stacked_from(): blocks = lax.all_gather(blocks, axes[k])  25.7 us
    reshape x2, local copies, waits for them, and re-layouts, in_order(): blocks.reshape(*shape[:dim], shape[dim] * shape[dim + 1], *shape[dim + 2:])  21.7 us
    concatenate x2, other arithmetic, gather_all_axes(): return in_order(jnp.concatenate(gathered, axis=widest + 1), dim)  13.5 us
    all_gather x2, local copies, waits for them, and re-layouts, stacked_from(): blocks = lax.all_gather(blocks, axes[k])  8.36 us
  transfers between devices with their start and end apart: 6, of which 5 were waited for; matrix products, arithmetic and copies ran while one was open for 9% of the time, Pallas kernels for 0%

commit v1 on v0

v1 whole, which is shorter than its diff:
```python
import functools

import jax
import jax.numpy as jnp
from jax import lax
from jax.experimental import pallas as pl
from jax.experimental.pallas import tpu as pltpu
from jax.sharding import Mesh
from jax.sharding import PartitionSpec as P

MESH = pl.DeviceIdType.MESH
AXES = ("y", "xl", "z", "xh", "c")
SHARD = ("y", "xl")
COLS = ("z", "xh", "c")
SIZES = (4, 2, 4, 2, 2)

mix_rate = 1.0

GROUP = 128
CHUNK = 64
PARTS = 7
DEPTH = 4
LINKS = ("up", "down", "across")


def plan_of(chunks):
    count = len(chunks)
    across_first = [k for k in range(count) if (k * 5) % 9 < 5]
    along_first = [k for k in range(count) if (k * 5) % 9 >= 5]

    def halves(ks):
        return ks[0::2], ks[1::2]

    p_up, p_down = halves(across_first)
    q_up, q_down = halves(along_first)
    up, down, across = [], [], []
    own, back, ahead, far = (0, 0), (3, 0), (1, 0), (2, 0)
    for k in along_first:
        up.append((own, back, k))
        down.append((own, ahead, k))
    for k in q_up:
        up.append((back, far, k))
    for k in q_down:
        down.append((ahead, far, k))
    for k in across_first:
        up.append((own, back, k))
        down.append((own, ahead, k))
    for k in across_first:
        up.append(((0, 1), (3, 1), k))
        down.append(((0, 1), (1, 1), k))
    for k in p_up:
        up.append((back, far, k))
    for k in p_down:
        down.append((ahead, far, k))
    for k in p_down:
        up.append(((3, 1), (2, 1), k))
    for k in p_up:
        down.append(((1, 1), (2, 1), k))
    for k in across_first:
        across.append((own, (0, 1), k))
    for k in along_first:
        across.append((own, (0, 1), k))
    for held in (back, ahead, far):
        for k in along_first:
            across.append((held, (held[0], 1), k))
    return up, down, across


def slot_of(owner):
    return owner[0] * 2 + owner[1] - 1


def kernel(
    train_gate, low_gate, high_gate, train_up, low_up, high_up, norm_train, norm_step,
    out_gate, out_up, out_norm,
    blocks, lows, highs, norms, gains, load_sems, small_sems, send_sems, recv_sems, gain_sends, gain_recvs,
):
    y, xl, z, xh, c = (lax.axis_index(name) for name in AXES)
    rows, width = train_gate.shape
    groups = width // GROUP
    outs = (out_gate, out_up)
    trains = (train_gate, train_up)

    small = [
        pltpu.make_async_copy(source, target, small_sems.at[k])
        for k, (source, target) in enumerate(
            (
                (low_gate, lows.at[0]), (high_gate, highs.at[0]), (low_up, lows.at[1]), (high_up, highs.at[1]),
                (norm_train, norms.at[0]), (norm_step, norms.at[1]),
            )
        )
    ]
    for copy in small:
        copy.start()
    loads = {}
    for g in range(groups):
        for m in range(2):
            loads[m, g] = pltpu.make_async_copy(
                trains[m].at[:, pl.ds(g * GROUP, GROUP)],
                blocks.at[m, :, pl.ds(g * GROUP, GROUP)],
                load_sems.at[m, g],
            )
            loads[m, g].start()

    def peer(**moved):
        return moved

    y_next, y_last, y_far = lax.rem(y + 1, 4), lax.rem(y + 3, 4), lax.rem(y + 2, 4)
    across_x = 1 - xl
    gain_peers = (
        (1, [peer(c=1 - c)]),
        (2, [peer(xh=1 - xh)]),
        (4, [peer(z=lax.rem(z + k, 4)) for k in (1, 3, 2)]),
        (16, [peer(xl=across_x)]),
        (32, [peer(y=y_next), peer(y=y_last), peer(y=y_far)]),
    )
    everyone = [p for _, peers in gain_peers for p in peers]
    barrier = pltpu.get_barrier_semaphore()
    for p in everyone:
        pl.semaphore_signal(barrier, inc=1, device_id=p, device_id_type=MESH)

    for copy in small:
        copy.wait()
    me = (y * 2 + xl) * 16 + (z * 2 + xh) * 2 + c
    gains[me] = jnp.zeros((1, 128), jnp.float32)
    gains[me, :, 0:32] = norms[0] + norms[1]

    def columns_of(owner):
        column = lax.rem(y + owner[0], 4) * 2 + (across_x if owner[1] else xl)
        return pl.ds(pl.multiple_of(column * rows, rows), rows)

    def merge(m, g):
        loads[m, g].wait()
        span = pl.ds(g * GROUP, GROUP)
        high = highs[m, :, span].astype(jnp.float32).T.astype(jnp.bfloat16)
        product = jnp.dot(high, lows[m], preferred_element_type=jnp.float32)
        latest = blocks[m, :, span].T.astype(jnp.float32) + mix_rate * product
        outs[m][span, columns_of((0, 0))] = latest.astype(jnp.bfloat16)

    per_group = GROUP // CHUNK
    chunks = [(m, g * GROUP + k * CHUNK) for g in range(groups) for m in range(2) for k in range(per_group)]
    merged = set()
    arrived = set()
    targets = (peer(y=y_next), peer(y=y_last), peer(xl=across_x))
    sent = ([], [], [])

    def window(owner, chunk):
        m, row = chunks[chunk]
        return outs[m].at[pl.ds(row, CHUNK), columns_of(owner)]

    def need(owner, chunk):
        if owner == (0, 0):
            m, row = chunks[chunk]
            if (m, row // GROUP) not in merged:
                merged.add((m, row // GROUP))
                merge(m, row // GROUP)
        elif (owner, chunk) not in arrived:
            arrived.add((owner, chunk))
            here = window(owner, chunk)
            pltpu.make_async_copy(here, here, recv_sems.at[slot_of(owner), chunk]).wait()

    def send(link, held, seen, chunk):
        order = len(sent[link])
        if order >= DEPTH:
            sent[link][order - DEPTH].wait_send()
        need(held, chunk)
        part = window(held, chunk)
        copy = pltpu.make_async_remote_copy(
            src_ref=part,
            dst_ref=part,
            send_sem=send_sems.at[link, order % DEPTH],
            recv_sem=recv_sems.at[slot_of(seen), chunk],
            device_id=targets[link],
            device_id_type=MESH,
        )
        copy.start()
        sent[link].append(copy)

    gain_copies = []

    def pass_gains(stage):
        for copy in gain_copies:
            copy.wait()
        gain_copies.clear()
        if stage == len(gain_peers):
            return
        count, peers = gain_peers[stage]
        first = me // count * count
        part = gains.at[pl.ds(first, count)]
        base = sum(len(p) for _, p in gain_peers[:stage])
        for k, p in enumerate(peers):
            copy = pltpu.make_async_remote_copy(
                src_ref=part,
                dst_ref=part,
                send_sem=gain_sends.at[base + k],
                recv_sem=gain_recvs.at[base + k],
                device_id=p,
                device_id_type=MESH,
            )
            copy.start()
            gain_copies.append(copy)

    links = plan_of(chunks)
    need(*links[0][0][0::2])
    need(*links[2][0][0::2])
    pl.semaphore_wait(barrier, len(everyone))
    steps = max(len(link) for link in links)
    stage = 0
    for step in range(steps):
        for link, items in enumerate(links):
            if step < len(items):
                send(link, *items[step])
        if step >= 12 and step % 6 == 0 and stage <= len(gain_peers):
            pass_gains(stage)
            stage += 1

    lane = lax.broadcasted_iota(jnp.int32, (1, 128), 1) // 32
    for r in range(32):
        row = gains[4 * r]
        for k in range(1, 4):
            row = jnp.where(lane == k, pltpu.roll(gains[4 * r + k], 32 * k, 1), row)
        out_norm[r : r + 1, :] = row

    for copies in sent:
        for copy in copies[-DEPTH:]:
            copy.wait_send()
    for oy in range(4):
        for ox in range(2):
            if (oy, ox) != (0, 0):
                for k in range(len(chunks)):
                    need((oy, ox), k)


def write_out(gate, up, gain, out_gate, out_up, out_gain, sems):
    step = gate.shape[0] // PARTS
    copies = []
    for k in range(PARTS):
        for m, (source, target) in enumerate(((gate, out_gate), (up, out_up))):
            part = pl.ds(k * step, step)
            copies.append(pltpu.make_async_copy(source.at[part], target.at[part], sems.at[m, k]))
            copies[-1].start()
    out_gain[...] = gain[...].astype(jnp.bfloat16)
    for copy in copies:
        copy.wait()


def per_device(train_gate, low_gate, high_gate, train_up, low_up, high_up, norm_train, norm_step):
    rows, width = train_gate.shape
    groups = width // GROUP
    chunk_count = 2 * width // CHUNK
    whole = rows * 8
    rank = low_gate.shape[1]
    vmem = pl.BlockSpec(memory_space=pltpu.VMEM)
    hbm = pl.BlockSpec(memory_space=pltpu.HBM)
    gathered = pl.pallas_call(
        kernel,
        out_shape=(
            jax.ShapeDtypeStruct((width, whole), jnp.bfloat16),
            jax.ShapeDtypeStruct((width, whole), jnp.bfloat16),
            jax.ShapeDtypeStruct((32, 128), jnp.float32),
        ),
        in_specs=[hbm] * 8,
        out_specs=(vmem, vmem, vmem),
        scratch_shapes=[
            pltpu.VMEM((2, rows, width), jnp.bfloat16),
            pltpu.VMEM((2, rank, rows), jnp.bfloat16),
            pltpu.VMEM((2, rank, width), jnp.bfloat16),
            pltpu.VMEM((2, 1, 32), jnp.float32),
            pltpu.VMEM((128, 1, 128), jnp.float32),
            pltpu.SemaphoreType.DMA((2, groups)),
            pltpu.SemaphoreType.DMA((6,)),
            pltpu.SemaphoreType.DMA((3, DEPTH)),
            pltpu.SemaphoreType.DMA((7, chunk_count)),
            pltpu.SemaphoreType.DMA((9,)),
            pltpu.SemaphoreType.DMA((9,)),
        ],
        compiler_params=pltpu.CompilerParams(
            collective_id=0, has_side_effects=True, vmem_limit_bytes=24 * 1024 * 1024
        ),
        cost_estimate=pl.CostEstimate(flops=10**9, bytes_accessed=2 * 10**7, transcendentals=0),
    )(
        *(
            pltpu.with_memory_space_constraint(x, pltpu.HBM)
            for x in (
                train_gate, low_gate.T, high_gate, train_up, low_up.T, high_up,
                norm_train.reshape(1, 32), norm_step.reshape(1, 32),
            )
        )
    )
    ready_gate, ready_up, gain = pl.pallas_call(
        write_out,
        out_shape=(
            jax.ShapeDtypeStruct((width, whole), jnp.bfloat16),
            jax.ShapeDtypeStruct((width, whole), jnp.bfloat16),
            jax.ShapeDtypeStruct((32, 128), jnp.bfloat16),
        ),
        in_specs=[vmem] * 3,
        out_specs=(hbm, hbm, vmem),
        scratch_shapes=[pltpu.SemaphoreType.DMA((2, PARTS))],
        compiler_params=pltpu.CompilerParams(vmem_limit_bytes=24 * 1024 * 1024),
        cost_estimate=pl.CostEstimate(flops=10**7, bytes_accessed=3 * 10**7, transcendentals=0),
    )(*gathered)
    return (ready_gate, ready_up, gain.reshape(-1))


def solution(mesh):
    finer = Mesh(mesh.devices.reshape(SIZES), AXES)
    placed = (
        P(SHARD, COLS),
        P(SHARD, None),
        P(None, COLS),
        P(SHARD, COLS),
        P(SHARD, None),
        P(None, COLS),
        P(SHARD + COLS),
        P(SHARD + COLS),
    )
    return jax.shard_map(
        per_device,
        mesh=finer,
        in_specs=placed,
        out_specs=(P(COLS, None), P(COLS, None), P()),
        check_vma=False,
    )
```

time: 302 us -> 110 us (0.36)
  waiting for transfers between devices: 146 us -> 0 us
  Pallas kernels: 0 us -> 109 us
  blocking collectives: 91.4 us -> 0 us
  local copies, waits for them, and re-layouts: 32.8 us -> 0 us
  between operations: 14.2 us -> 0.64 us
  other arithmetic: 13.5 us -> 0 us
    all_gather x6 -> x0, waiting for transfers between devices: 146 us -> none  [stacked_from(): blocks = lax.all_gather(blocks, axes[k])]
    pallas_call x0 -> x2, Pallas kernels: none -> 109 us  [the longest x1 103 us: per_device(): pl.pallas_call(kernel, out_shape=(jax.ShapeDtypeStruct((width, whole), jn...]
    unnamed x1 -> x0, blocking collectives: 65.6 us -> none
    all_gather x2 -> x0, blocking collectives: 25.7 us -> none  [stacked_from(): blocks = lax.all_gather(blocks, axes[k])]
    reshape x2 -> x0, local copies, waits for them, and re-layouts: 21.7 us -> none  [in_order(): blocks.reshape(*shape[:dim], shape[dim] * shape[dim + 1], *shape[dim + 2:])]
    concatenate x2 -> x0, other arithmetic: 13.5 us -> none  [gather_all_axes(): return in_order(jnp.concatenate(gathered, axis=widest + 1), dim)]
    all_gather x2 -> x0, local copies, waits for them, and re-layouts: 8.36 us -> none  [stacked_from(): blocks = lax.all_gather(blocks, axes[k])]
  transfers between devices with their start and end apart: 6 -> 0, of which waited for: 5 -> 0; matrix products, arithmetic and copies ran while one was open for 9% -> 0% of each run, Pallas kernels for 0% -> 0%
where the time goes in v1:
time: 110 us
  Pallas kernels  109 us (99%)
    pallas_call x1, Pallas kernels, per_device(): pl.pallas_call(kernel, out_shape=(jax.ShapeDtypeStruct((width, whole), jn...  103 us
    pallas_call x1, Pallas kernels, per_device(): pl.pallas_call(write_out, out_shape=(jax.ShapeDtypeStruct((width, whole),...  5.91 us

profile of v1, /device:TPU:0, one launch (start us, length us, event | category | flops | bytes accessed | tf_op | source)
XLA Modules:
  0.0 109.9 jit_solution(8534583312710870732)
XLA Ops:
  0.6 103.3 %shard_map.103 = (bf16[896,4096]{1,0:T(8,128)(2,1)S(1)}, bf16[896,4096]{1,0:T(8,128)(2,1)S(1)}, f32[32,128]{1,0:T(8,128)S(1)}) custom-call(bf16[512,896]{1,0:T(8,128)(2,1)} %train_gate.1, bf16[32,512]{1,0:T(8,128)(2,1)} %bitcast.5, bf16[32,896]{1,0:T(8,128)(2,1)} %high_gate.1, bf16[512,896]{1,0:T(8,128)(2,1)} %train_up.1, bf16[32,512]{1,0:T(8,128)(2,1)} %bitcast.6, ...), custom_call_target="tpu_custom_call" | custom-call | flops 1000000000 | bytes 20000000 | tf_op jit(solution)/shard_map/pallas_call | solution.py:255
  104.0 5.9 %shard_map.104 = (bf16[896,4096]{1,0:T(8,128)(2,1)}, bf16[896,4096]{1,0:T(8,128)(2,1)}, bf16[32,128]{1,0:T(8,128)(2,1)}) custom-call(bf16[896,4096]{1,0:T(8,128)(2,1)S(1)} %get-tuple-element.9.gate, bf16[896,4096]{1,0:T(8,128)(2,1)S(1)} %get-tuple-element.10.up, f32[32,128]{1,0:T(8,128)S(1)} %get-tuple-element.11.gain), custom_call_target="tpu_custom_call" | custom-call | flops 10000000 | bytes 30000000 | tf_op jit(solution)/shard_map/pallas_call | solution.py:290

commit v2 on v1

v2 whole, which is shorter than its diff:
```python
import functools

import jax
import jax.numpy as jnp
from jax import lax
from jax.experimental import pallas as pl
from jax.experimental.pallas import tpu as pltpu
from jax.sharding import Mesh
from jax.sharding import PartitionSpec as P

MESH = pl.DeviceIdType.MESH
AXES = ("y", "xl", "z", "xh", "c")
SHARD = ("y", "xl")
COLS = ("z", "xh", "c")
SIZES = (4, 2, 4, 2, 2)

mix_rate = 1.0

GROUP = 128
CHUNK = 64
SPANS = ((0, 1), (1, 2), (3, 4))
PARTS = 7
DEPTH = 4

OWN, BACK, AHEAD, FAR = (0, 0), (3, 0), (1, 0), (2, 0)


def chunks_of(groups):
    pieces = [(m, g * GROUP + k, CHUNK) for g in range(groups) for m in range(2) for k in range(0, GROUP, CHUNK)]
    kinds = ([], [])
    for k, piece in enumerate(pieces):
        kinds[0 if (k * 5) % 9 < 5 else 1].append(piece)
    m, row, rows = kinds[0].pop()
    kinds[0].append((m, row, rows // 2))
    kinds[1].append((m, row + rows // 2, rows // 2))
    return kinds


def plan_of(kinds):
    first, second = kinds
    up, down, across = [], [], []

    def add(link, held, seen, kind, pieces):
        link.extend((held, seen, kind, piece) for piece in pieces)

    for kind in (1, 0):
        add(up, OWN, BACK, kind, kinds[kind])
        add(down, OWN, AHEAD, kind, kinds[kind])
    add(up, BACK, FAR, 1, second[0::2])
    add(down, AHEAD, FAR, 1, second[1::2])
    add(up, (0, 1), (3, 1), 0, first)
    add(down, (0, 1), (1, 1), 0, first)
    add(up, BACK, FAR, 0, first[0::2])
    add(down, AHEAD, FAR, 0, first[1::2])
    add(up, (3, 1), (2, 1), 0, first[1::2])
    add(down, (1, 1), (2, 1), 0, first[0::2])
    add(across, OWN, (0, 1), 0, first)
    for held in (OWN, BACK, AHEAD, FAR):
        add(across, held, (held[0], 1), 1, second)
    return up, down, across


def in_turn(links):
    places, loads = [0] * len(links), [0] * len(links)
    while any(place < len(link) for place, link in zip(places, links)):
        k = min((loads[k], k) for k in range(len(links)) if places[k] < len(links[k]))[1]
        item = links[k][places[k]]
        yield (k, *item)
        places[k] += 1
        loads[k] += item[-1][2]


def kernel(
    train_gate, low_gate, high_gate, train_up, low_up, high_up, norm_train, norm_step,
    out_gate, out_up, out_norm,
    blocks, lows, highs, norms, gains, load_sems, small_sems, send_sems, recv_sems, gain_sends, gain_recvs,
):
    y, xl, z, xh, c = (lax.axis_index(name) for name in AXES)
    rows, width = train_gate.shape
    groups = width // GROUP
    outs = (out_gate, out_up)

    y_next, y_last, y_far = lax.rem(y + 1, 4), lax.rem(y + 3, 4), lax.rem(y + 2, 4)
    across_x = 1 - xl
    gain_peers = (
        (1, [{"c": 1 - c}]),
        (2, [{"xh": 1 - xh}]),
        (4, [{"z": lax.rem(z + k, 4)} for k in (1, 3, 2)]),
        (16, [{"xl": across_x}]),
        (32, [{"y": y_next}, {"y": y_last}, {"y": y_far}]),
    )
    everyone = [p for _, peers in gain_peers for p in peers]
    barrier = pltpu.get_barrier_semaphore()
    for p in everyone:
        pl.semaphore_signal(barrier, inc=1, device_id=p, device_id_type=MESH)

    sources = ((train_gate, low_gate, high_gate), (train_up, low_up, high_up))
    loads = {}
    for s, (first, count) in enumerate(SPANS):
        span = pl.ds(first * GROUP, count * GROUP)
        for m, (train, low, high) in enumerate(sources):
            if s == 0:
                loads[m, "high"] = pltpu.make_async_copy(high, highs.at[m], small_sems.at[m, 0])
                loads[m, "low"] = pltpu.make_async_copy(low, lows.at[m], small_sems.at[m, 1])
                loads[m, "high"].start()
                loads[m, "low"].start()
            loads[m, first] = pltpu.make_async_copy(train.at[:, span], blocks.at[m, :, span], load_sems.at[m, s])
            loads[m, first].start()
    for k, norm in enumerate((norm_train, norm_step)):
        pltpu.make_async_copy(norm, norms.at[k], small_sems.at[2, 0]).start()

    def columns_of(owner):
        column = lax.rem(y + owner[0], 4) * 2 + (across_x if owner[1] else xl)
        return pl.ds(pl.multiple_of(column * rows, rows), rows)

    def merge(m, g):
        if g == 0:
            loads[m, "high"].wait()
            loads[m, "low"].wait()
        if (m, g) in loads:
            loads[m, g].wait()
        span = pl.ds(g * GROUP, GROUP)
        high = highs[m, :, span].astype(jnp.float32).T.astype(jnp.bfloat16)
        product = jnp.dot(high, lows[m], preferred_element_type=jnp.float32)
        latest = blocks[m, :, span].T.astype(jnp.float32) + mix_rate * product
        outs[m][span, columns_of(OWN)] = latest.astype(jnp.bfloat16)

    kinds = chunks_of(groups)
    totals = [sum(piece[2] for piece in pieces) for pieces in kinds]
    merged, arrived = set(), set()
    targets = ({"y": y_next}, {"y": y_last}, {"xl": across_x})
    sent = ([], [], [])

    def merge_piece(piece):
        at = (piece[0], piece[1] // GROUP)
        if at not in merged:
            merged.add(at)
            merge(*at)

    def receive(owner, kind):
        if (owner, kind) not in arrived:
            arrived.add((owner, kind))
            as_many = out_gate.at[pl.ds(0, totals[kind] // 2), pl.ds(0, 2 * rows)]
            sem = recv_sems.at[owner[0] * 2 + owner[1] - 1, kind]
            pltpu.make_async_copy(as_many, as_many, sem).wait()

    def send(link, held, seen, kind, piece):
        order = len(sent[link])
        if order >= DEPTH:
            sent[link][order - DEPTH].wait_send()
        if held == OWN:
            merge_piece(piece)
        else:
            receive(held, kind)
        m, row, count = piece
        part = outs[m].at[pl.ds(row, count), columns_of(held)]
        copy = pltpu.make_async_remote_copy(
            src_ref=part,
            dst_ref=part,
            send_sem=send_sems.at[link, order % DEPTH],
            recv_sem=recv_sems.at[seen[0] * 2 + seen[1] - 1, kind],
            device_id=targets[link],
            device_id_type=MESH,
        )
        copy.start()
        sent[link].append(copy)

    me = (y * 2 + xl) * 16 + (z * 2 + xh) * 2 + c

    def pass_gains(stage):
        if stage == 0:
            pltpu.make_async_copy(norms, norms, small_sems.at[2, 0]).wait()
            gains[me] = jnp.zeros((1, 128), jnp.float32)
            gains[me, :, 0:32] = norms[0] + norms[1]
            return
        if stage > 1:
            count, peers = gain_peers[stage - 2]
            as_many = gains.at[pl.ds(0, count * len(peers))]
            pltpu.make_async_copy(as_many, as_many, gain_sends.at[stage - 2]).wait()
            pltpu.make_async_copy(as_many, as_many, gain_recvs.at[stage - 2]).wait()
        if stage <= len(gain_peers):
            count, peers = gain_peers[stage - 1]
            part = gains.at[pl.ds(me // count * count, count)]
            for p in peers:
                pltpu.make_async_remote_copy(
                    src_ref=part,
                    dst_ref=part,
                    send_sem=gain_sends.at[stage - 1],
                    recv_sem=gain_recvs.at[stage - 1],
                    device_id=p,
                    device_id_type=MESH,
                ).start()

    merge_piece(kinds[1][0])
    merge_piece(kinds[0][0])
    pl.semaphore_wait(barrier, len(everyone))
    stage = 0
    for order, item in enumerate(in_turn(plan_of(kinds))):
        send(*item)
        if order >= 30 and order % 18 == 0 and stage <= len(gain_peers) + 1:
            pass_gains(stage)
            stage += 1

    lane = lax.broadcasted_iota(jnp.int32, (1, 128), 1) // 32
    for r in range(32):
        row = gains[4 * r]
        for k in range(1, 4):
            row = jnp.where(lane == k, pltpu.roll(gains[4 * r + k], 32 * k, 1), row)
        out_norm[r : r + 1, :] = row

    for copies in sent:
        for copy in copies[-DEPTH:]:
            copy.wait_send()
    for oy in range(4):
        for ox in range(2):
            if (oy, ox) != OWN:
                receive((oy, ox), 0)
                receive((oy, ox), 1)


def write_out(gate, up, gain, out_gate, out_up, out_gain, sems):
    step = gate.shape[0] // PARTS
    pairs = ((gate, out_gate), (up, out_up))
    for k in range(PARTS):
        part = pl.ds(k * step, step)
        for m, (source, target) in enumerate(pairs):
            pltpu.make_async_copy(source.at[part], target.at[part], sems.at[m]).start()
    out_gain[...] = gain[...].astype(jnp.bfloat16)
    for m, (source, target) in enumerate(pairs):
        pltpu.make_async_copy(source, target, sems.at[m]).wait()


def per_device(train_gate, low_gate, high_gate, train_up, low_up, high_up, norm_train, norm_step):
    rows, width = train_gate.shape
    whole = rows * 8
    rank = low_gate.shape[1]
    vmem = pl.BlockSpec(memory_space=pltpu.VMEM)
    hbm = pl.BlockSpec(memory_space=pltpu.HBM)
    gathered = pl.pallas_call(
        kernel,
        out_shape=(
            jax.ShapeDtypeStruct((width, whole), jnp.bfloat16),
            jax.ShapeDtypeStruct((width, whole), jnp.bfloat16),
            jax.ShapeDtypeStruct((32, 128), jnp.float32),
        ),
        in_specs=[hbm] * 8,
        out_specs=(vmem, vmem, vmem),
        scratch_shapes=[
            pltpu.VMEM((2, rows, width), jnp.bfloat16),
            pltpu.VMEM((2, rank, rows), jnp.bfloat16),
            pltpu.VMEM((2, rank, width), jnp.bfloat16),
            pltpu.VMEM((2, 1, 32), jnp.float32),
            pltpu.VMEM((128, 1, 128), jnp.float32),
            pltpu.SemaphoreType.DMA((2, len(SPANS))),
            pltpu.SemaphoreType.DMA((3, 2)),
            pltpu.SemaphoreType.DMA((3, DEPTH)),
            pltpu.SemaphoreType.DMA((7, 2)),
            pltpu.SemaphoreType.DMA((5,)),
            pltpu.SemaphoreType.DMA((5,)),
        ],
        compiler_params=pltpu.CompilerParams(
            collective_id=0, has_side_effects=True, vmem_limit_bytes=24 * 1024 * 1024
        ),
        cost_estimate=pl.CostEstimate(flops=10**9, bytes_accessed=2 * 10**7, transcendentals=0),
    )(
        *(
            pltpu.with_memory_space_constraint(x, pltpu.HBM)
            for x in (
                train_gate, low_gate.T, high_gate, train_up, low_up.T, high_up,
                norm_train.reshape(1, 32), norm_step.reshape(1, 32),
            )
        )
    )
    ready_gate, ready_up, gain = pl.pallas_call(
        write_out,
        out_shape=(
            jax.ShapeDtypeStruct((width, whole), jnp.bfloat16),
            jax.ShapeDtypeStruct((width, whole), jnp.bfloat16),
            jax.ShapeDtypeStruct((32, 128), jnp.bfloat16),
        ),
        in_specs=[vmem] * 3,
        out_specs=(hbm, hbm, vmem),
        scratch_shapes=[pltpu.SemaphoreType.DMA((2,))],
        compiler_params=pltpu.CompilerParams(vmem_limit_bytes=24 * 1024 * 1024),
        cost_estimate=pl.CostEstimate(flops=10**7, bytes_accessed=3 * 10**7, transcendentals=0),
    )(*gathered)
    return (ready_gate, ready_up, gain.reshape(-1))


def solution(mesh):
    finer = Mesh(mesh.devices.reshape(SIZES), AXES)
    placed = (
        P(SHARD, COLS),
        P(SHARD, None),
        P(None, COLS),
        P(SHARD, COLS),
        P(SHARD, None),
        P(None, COLS),
        P(SHARD + COLS),
        P(SHARD + COLS),
    )
    return jax.shard_map(
        per_device,
        mesh=finer,
        in_specs=placed,
        out_specs=(P(COLS, None), P(COLS, None), P()),
        check_vma=False,
    )
```

time: 110 us -> 107 us (0.973)
  Pallas kernels: 109 us -> 107 us
    pallas_call x1, Pallas kernels: 103 us -> 101 us  [per_device(): pl.pallas_call(kernel, out_shape=(jax.ShapeDtypeStruct((width, whole), jn...]
where the time goes in v2:
time: 107 us
  Pallas kernels  107 us (100%)
    pallas_call x1, Pallas kernels, per_device(): pl.pallas_call(kernel, out_shape=(jax.ShapeDtypeStruct((width, whole), jn...  101 us
    pallas_call x1, Pallas kernels, per_device(): pl.pallas_call(write_out, out_shape=(jax.ShapeDtypeStruct((width, whole),...  5.8 us

profile of v2, /device:TPU:0, one launch (start us, length us, event | category | flops | bytes accessed | tf_op | source)
XLA Modules:
  0.0 107.3 jit_solution(10255284800771087162)
XLA Ops:
  0.6 100.8 %shard_map.103 = (bf16[896,4096]{1,0:T(8,128)(2,1)S(1)}, bf16[896,4096]{1,0:T(8,128)(2,1)S(1)}, f32[32,128]{1,0:T(8,128)S(1)}) custom-call(bf16[512,896]{1,0:T(8,128)(2,1)} %train_gate.1, bf16[32,512]{1,0:T(8,128)(2,1)} %bitcast.5, bf16[32,896]{1,0:T(8,128)(2,1)} %high_gate.1, bf16[512,896]{1,0:T(8,128)(2,1)} %train_up.1, bf16[32,512]{1,0:T(8,128)(2,1)} %bitcast.6, ...), custom_call_target="tpu_custom_call" | custom-call | flops 1000000000 | bytes 20000000 | tf_op jit(solution)/shard_map/pallas_call | solution.py:239
  101.5 5.8 %shard_map.104 = (bf16[896,4096]{1,0:T(8,128)(2,1)}, bf16[896,4096]{1,0:T(8,128)(2,1)}, bf16[32,128]{1,0:T(8,128)(2,1)}) custom-call(bf16[896,4096]{1,0:T(8,128)(2,1)S(1)} %get-tuple-element.9.gate, bf16[896,4096]{1,0:T(8,128)(2,1)S(1)} %get-tuple-element.10.up, f32[32,128]{1,0:T(8,128)S(1)} %get-tuple-element.11.gain), custom_call_target="tpu_custom_call" | custom-call | flops 10000000 | bytes 30000000 | tf_op jit(solution)/shard_map/pallas_call | solution.py:274

commit v3 on v2

--- a/solution.py
+++ b/solution.py
@@ -73,26 +73,25 @@
 def kernel(
     train_gate, low_gate, high_gate, train_up, low_up, high_up, norm_train, norm_step,
     out_gate, out_up, out_norm,
-    blocks, lows, highs, norms, gains, load_sems, small_sems, send_sems, recv_sems, gain_sends, gain_recvs,
+    blocks, lows, highs, norms, own_gain, gains, load_sems, small_sems, send_sems, recv_sems, gain_sends, gain_recvs, ready,
 ):
     y, xl, z, xh, c = (lax.axis_index(name) for name in AXES)
     rows, width = train_gate.shape
     groups = width // GROUP
     outs = (out_gate, out_up)
 
-    y_next, y_last, y_far = lax.rem(y + 1, 4), lax.rem(y + 3, 4), lax.rem(y + 2, 4)
+    y_next, y_last = lax.rem(y + 1, 4), lax.rem(y + 3, 4)
     across_x = 1 - xl
-    gain_peers = (
-        (1, [{"c": 1 - c}]),
-        (2, [{"xh": 1 - xh}]),
-        (4, [{"z": lax.rem(z + k, 4)} for k in (1, 3, 2)]),
-        (16, [{"xl": across_x}]),
-        (32, [{"y": y_next}, {"y": y_last}, {"y": y_far}]),
-    )
-    everyone = [p for _, peers in gain_peers for p in peers]
+    targets = ({"y": y_next}, {"y": y_last}, {"xl": across_x})
+    greeter = lax.rem(y + xl, 2) == 1
+    answerer = jnp.logical_not(greeter)
+    far_peers = [{"c": 1 - c}, {"xh": 1 - xh}] + [{"z": lax.rem(z + k, 4)} for k in (1, 3, 2)]
     barrier = pltpu.get_barrier_semaphore()
-    for p in everyone:
-        pl.semaphore_signal(barrier, inc=1, device_id=p, device_id_type=MESH)
+
+    @pl.when(greeter)
+    def _():
+        for p in (*targets, *far_peers):
+            pl.semaphore_signal(barrier, inc=1, device_id=p, device_id_type=MESH)
 
     sources = ((train_gate, low_gate, high_gate), (train_up, low_up, high_up))
     loads = {}
@@ -128,7 +127,6 @@
     kinds = chunks_of(groups)
     totals = [sum(piece[2] for piece in pieces) for pieces in kinds]
     merged, arrived = set(), set()
-    targets = ({"y": y_next}, {"y": y_last}, {"xl": across_x})
     sent = ([], [], [])
 
     def merge_piece(piece):
@@ -165,47 +163,85 @@
         copy.start()
         sent[link].append(copy)
 
-    me = (y * 2 + xl) * 16 + (z * 2 + xh) * 2 + c
-
-    def pass_gains(stage):
-        if stage == 0:
+    col = (z * 2 + xh) * 2 + c
+    me = y * 32 + col * 2 + xl
+    gain_steps = (
+        (answerer, me, 1, targets[2:], greeter),
+        (greeter, me // 2 * 2, 2, far_peers[:1], greeter),
+        (greeter, me // 4 * 4, 4, far_peers[1:2], greeter),
+        (greeter, me // 8 * 8, 8, far_peers[2:], greeter),
+        (greeter, y * 32, 32, targets[2:], answerer),
+        (None, y * 32, 32, targets[:2], None),
+        (None, y_last * 32, 32, targets[:1], None),
+    )
+
+    def only(condition, act):
+        if condition is None:
+            act()
+        else:
+            pl.when(condition)(act)
+
+    def pass_gains(step):
+        if step == 0:
             pltpu.make_async_copy(norms, norms, small_sems.at[2, 0]).wait()
-            gains[me] = jnp.zeros((1, 128), jnp.float32)
-            gains[me, :, 0:32] = norms[0] + norms[1]
+            own_gain[...] = jnp.zeros((1, 1, 128), jnp.float32)
+            own_gain[0, :, 0:32] = norms[0] + norms[1]
+
+            @pl.when(greeter)
+            def _():
+                gains[me] = own_gain[0]
+
             return
-        if stage > 1:
-            count, peers = gain_peers[stage - 2]
+        if step > 1:
+            senders, _, count, peers, receivers = gain_steps[step - 2]
             as_many = gains.at[pl.ds(0, count * len(peers))]
-            pltpu.make_async_copy(as_many, as_many, gain_sends.at[stage - 2]).wait()
-            pltpu.make_async_copy(as_many, as_many, gain_recvs.at[stage - 2]).wait()
-        if stage <= len(gain_peers):
-            count, peers = gain_peers[stage - 1]
-            part = gains.at[pl.ds(me // count * count, count)]
-            for p in peers:
-                pltpu.make_async_remote_copy(
-                    src_ref=part,
-                    dst_ref=part,
-                    send_sem=gain_sends.at[stage - 1],
-                    recv_sem=gain_recvs.at[stage - 1],
-                    device_id=p,
-                    device_id_type=MESH,
-                ).start()
+            only(senders, pltpu.make_async_copy(as_many, as_many, gain_sends.at[step - 2]).wait)
+            only(receivers, pltpu.make_async_copy(as_many, as_many, gain_recvs.at[step - 2]).wait)
+        if step == 2:
+            only(greeter, lambda: pl.semaphore_wait(barrier, len(far_peers)))
+        if step <= len(gain_steps):
+            senders, first, count, peers, _ = gain_steps[step - 1]
+            part = gains.at[pl.ds(first, count)]
+
+            def start():
+                for p in peers:
+                    pltpu.make_async_remote_copy(
+                        src_ref=own_gain if step == 1 else part,
+                        dst_ref=part,
+                        send_sem=gain_sends.at[step - 1],
+                        recv_sem=gain_recvs.at[step - 1],
+                        device_id=p,
+                        device_id_type=MESH,
+                    ).start()
+
+            only(senders, start)
+
+    @pl.when(answerer)
+    def _():
+        pl.semaphore_wait(barrier, len(targets))
+        for p in targets:
+            pl.semaphore_signal(ready, inc=1, device_id=p, device_id_type=MESH)
 
     merge_piece(kinds[1][0])
     merge_piece(kinds[0][0])
-    pl.semaphore_wait(barrier, len(everyone))
-    stage = 0
+
+    @pl.when(greeter)
+    def _():
+        pl.semaphore_wait(ready, len(targets))
+
+    step = 0
     for order, item in enumerate(in_turn(plan_of(kinds))):
         send(*item)
-        if order >= 30 and order % 18 == 0 and stage <= len(gain_peers) + 1:
-            pass_gains(stage)
-            stage += 1
+        if order >= 24 and order % 18 == 6 and step <= len(gain_steps) + 1:
+            pass_gains(step)
+            step += 1
 
     lane = lax.broadcasted_iota(jnp.int32, (1, 128), 1) // 32
     for r in range(32):
-        row = gains[4 * r]
+        first = r // 8 * 32 + r % 4 * 8 + r // 4 % 2
+        row = gains[first]
         for k in range(1, 4):
-            row = jnp.where(lane == k, pltpu.roll(gains[4 * r + k], 32 * k, 1), row)
+            row = jnp.where(lane == k, pltpu.roll(gains[first + 2 * k], 32 * k, 1), row)
         out_norm[r : r + 1, :] = row
 
     for copies in sent:
@@ -250,13 +286,15 @@
             pltpu.VMEM((2, rank, rows), jnp.bfloat16),
             pltpu.VMEM((2, rank, width), jnp.bfloat16),
             pltpu.VMEM((2, 1, 32), jnp.float32),
+            pltpu.VMEM((1, 1, 128), jnp.float32),
             pltpu.VMEM((128, 1, 128), jnp.float32),
             pltpu.SemaphoreType.DMA((2, len(SPANS))),
             pltpu.SemaphoreType.DMA((3, 2)),
             pltpu.SemaphoreType.DMA((3, DEPTH)),
             pltpu.SemaphoreType.DMA((7, 2)),
-            pltpu.SemaphoreType.DMA((5,)),
-            pltpu.SemaphoreType.DMA((5,)),
+            pltpu.SemaphoreType.DMA((7,)),
+            pltpu.SemaphoreType.DMA((7,)),
+            pltpu.SemaphoreType.REGULAR,
         ],
         compiler_params=pltpu.CompilerParams(
             collective_id=0, has_side_effects=True, vmem_limit_bytes=24 * 1024 * 1024

time: 107 us -> 106 us (level)
  no operation moved by 1% of the time
where the time goes in v3:
time: 106 us
  Pallas kernels  106 us (100%)
    pallas_call x1, Pallas kernels, per_device(): pl.pallas_call(kernel, out_shape=(jax.ShapeDtypeStruct((width, whole), jn...  99.8 us
    pallas_call x1, Pallas kernels, per_device(): pl.pallas_call(write_out, out_shape=(jax.ShapeDtypeStruct((width, whole),...  5.8 us

profile of v3, /device:TPU:0, one launch (start us, length us, event | category | flops | bytes accessed | tf_op | source)
XLA Modules:
  0.0 106.2 jit_solution(11163548314739522918)
XLA Ops:
  0.6 99.8 %shard_map.103 = (bf16[896,4096]{1,0:T(8,128)(2,1)S(1)}, bf16[896,4096]{1,0:T(8,128)(2,1)S(1)}, f32[32,128]{1,0:T(8,128)S(1)}) custom-call(bf16[512,896]{1,0:T(8,128)(2,1)} %train_gate.1, bf16[32,512]{1,0:T(8,128)(2,1)} %bitcast.5, bf16[32,896]{1,0:T(8,128)(2,1)} %high_gate.1, bf16[512,896]{1,0:T(8,128)(2,1)} %train_up.1, bf16[32,512]{1,0:T(8,128)(2,1)} %bitcast.6, ...), custom_call_target="tpu_custom_call" | custom-call | flops 1000000000 | bytes 20000000 | tf_op jit(solution)/shard_map/pallas_call | solution.py:275
  100.4 5.8 %shard_map.104 = (bf16[896,4096]{1,0:T(8,128)(2,1)}, bf16[896,4096]{1,0:T(8,128)(2,1)}, bf16[32,128]{1,0:T(8,128)(2,1)}) custom-call(bf16[896,4096]{1,0:T(8,128)(2,1)S(1)} %get-tuple-element.9.gate, bf16[896,4096]{1,0:T(8,128)(2,1)S(1)} %get-tuple-element.10.up, f32[32,128]{1,0:T(8,128)S(1)} %get-tuple-element.11.gain), custom_call_target="tpu_custom_call" | custom-call | flops 10000000 | bytes 30000000 | tf_op jit(solution)/shard_map/pallas_call | solution.py:312

commit v4 on v3

--- a/solution.py
+++ b/solution.py
@@ -73,7 +73,7 @@
 def kernel(
     train_gate, low_gate, high_gate, train_up, low_up, high_up, norm_train, norm_step,
     out_gate, out_up, out_norm,
-    blocks, lows, highs, norms, own_gain, gains, load_sems, small_sems, send_sems, recv_sems, gain_sends, gain_recvs, ready,
+    blocks, lows, highs, norms, gains, packed, load_sems, small_sems, send_sems, recv_sems, gain_sends, gain_recvs, ready,
 ):
     y, xl, z, xh, c = (lax.axis_index(name) for name in AXES)
     rows, width = train_gate.shape
@@ -83,15 +83,28 @@
     y_next, y_last = lax.rem(y + 1, 4), lax.rem(y + 3, 4)
     across_x = 1 - xl
     targets = ({"y": y_next}, {"y": y_last}, {"xl": across_x})
-    greeter = lax.rem(y + xl, 2) == 1
-    answerer = jnp.logical_not(greeter)
-    far_peers = [{"c": 1 - c}, {"xh": 1 - xh}] + [{"z": lax.rem(z + k, 4)} for k in (1, 3, 2)]
+    neighbours = ((y_next, xl), (y_last, xl), (y, across_x))
+
+    def at_gate(yy, xx):
+        return jnp.logical_and(yy == 1, xx == 0)
+
+    hub_group = jnp.logical_and(xh == 1, c == 1)
+    gate = at_gate(y, xl)
+    hub = jnp.logical_and(gate, hub_group)
+    speaker = jnp.logical_and(gate, jnp.logical_not(hub_group))
+    nearby = [jnp.logical_and(hub_group, at_gate(*place)) for place in neighbours]
+    other_hubs = [{"z": lax.rem(z + k, 4)} for k in (1, 3, 2)]
+    speakers = [{"c": 0}, {"xh": 0}, {"xh": 0, "c": 0}]
     barrier = pltpu.get_barrier_semaphore()
 
-    @pl.when(greeter)
-    def _():
-        for p in (*targets, *far_peers):
-            pl.semaphore_signal(barrier, inc=1, device_id=p, device_id_type=MESH)
+    def greet(sem, *peers):
+        for p in peers:
+            pl.semaphore_signal(sem, inc=1, device_id=p, device_id_type=MESH)
+
+    for target, is_hub in zip(targets, nearby):
+        pl.when(jnp.logical_not(is_hub))(functools.partial(greet, barrier, target))
+    pl.when(hub)(functools.partial(greet, barrier, *other_hubs))
+    pl.when(speaker)(functools.partial(greet, barrier, {"xh": 1, "c": 1}))
 
     sources = ((train_gate, low_gate, high_gate), (train_up, low_up, high_up))
     loads = {}
@@ -164,15 +177,17 @@
         sent[link].append(copy)
 
     col = (z * 2 + xh) * 2 + c
-    me = y * 32 + col * 2 + xl
+    me = col * 8 + y * 2 + xl
     gain_steps = (
-        (answerer, me, 1, targets[2:], greeter),
-        (greeter, me // 2 * 2, 2, far_peers[:1], greeter),
-        (greeter, me // 4 * 4, 4, far_peers[1:2], greeter),
-        (greeter, me // 8 * 8, 8, far_peers[2:], greeter),
-        (greeter, y * 32, 32, targets[2:], answerer),
-        (None, y * 32, 32, targets[:2], None),
-        (None, y_last * 32, 32, targets[:1], None),
+        (None, gains.at[pl.ds(me, 1)], targets[2:], None, 1),
+        (None, gains.at[pl.ds(me // 2 * 2, 2)], targets[:2], None, 4),
+        (None, gains.at[pl.ds(col * 8 + y_last * 2, 2)], targets[:1], None, 2),
+        (speaker, gains.at[pl.ds(col * 8, 8)], [{"xh": 1, "c": 1}], hub, 24),
+        (hub, gains.at[pl.ds(z * 32, 32)], other_hubs, hub, 96),
+        (hub, out_norm, speakers, speaker, 16),
+        (gate, out_norm, targets[2:], jnp.logical_and(y == 1, xl == 1), 16),
+        (y == 1, out_norm, targets[:2], jnp.logical_or(y == 0, y == 2), 16),
+        (y == 2, out_norm, targets[:1], y == 3, 16),
     )
 
     def only(condition, act):
@@ -181,32 +196,47 @@
         else:
             pl.when(condition)(act)
 
+    def settle(sem, count):
+        as_many = gains.at[pl.ds(0, count)]
+        pltpu.make_async_copy(as_many, as_many, sem).wait()
+
+    def pack():
+        lane = lax.broadcasted_iota(jnp.int32, (1, 128), 1) // 32
+        for r in range(32):
+            first = r % 4 * 32 + r // 4
+            row = gains[first]
+            for k in range(1, 4):
+                row = jnp.where(lane == k, pltpu.roll(gains[first + 8 * k], 32 * k, 1), row)
+            packed[r : r + 1, :] = row
+        out_norm[...] = packed[...].astype(jnp.bfloat16)
+
+    def meet():
+        pl.semaphore_wait(barrier, len(other_hubs) + len(speakers))
+        greet(ready, *speakers)
+
     def pass_gains(step):
         if step == 0:
             pltpu.make_async_copy(norms, norms, small_sems.at[2, 0]).wait()
-            own_gain[...] = jnp.zeros((1, 1, 128), jnp.float32)
-            own_gain[0, :, 0:32] = norms[0] + norms[1]
-
-            @pl.when(greeter)
-            def _():
-                gains[me] = own_gain[0]
-
+            gains[me] = jnp.zeros((1, 128), jnp.float32)
+            gains[me, :, 0:32] = norms[0] + norms[1]
+            only(hub, meet)
             return
         if step > 1:
-            senders, _, count, peers, receivers = gain_steps[step - 2]
-            as_many = gains.at[pl.ds(0, count * len(peers))]
-            only(senders, pltpu.make_async_copy(as_many, as_many, gain_sends.at[step - 2]).wait)
-            only(receivers, pltpu.make_async_copy(as_many, as_many, gain_recvs.at[step - 2]).wait)
-        if step == 2:
-            only(greeter, lambda: pl.semaphore_wait(barrier, len(far_peers)))
+            senders, part, peers, receivers, received = gain_steps[step - 2]
+            count = 16 if part is out_norm else part.shape[0]
+            only(senders, functools.partial(settle, gain_sends.at[step - 2], count * len(peers)))
+            only(receivers, functools.partial(settle, gain_recvs.at[step - 2], received))
         if step <= len(gain_steps):
-            senders, first, count, peers, _ = gain_steps[step - 1]
-            part = gains.at[pl.ds(first, count)]
+            senders, part, peers, _, _ = gain_steps[step - 1]
 
             def start():
+                if step == 4:
+                    pl.semaphore_wait(ready, 1)
+                if step == 6:
+                    pack()
                 for p in peers:
                     pltpu.make_async_remote_copy(
-                        src_ref=own_gain if step == 1 else part,
+                        src_ref=part,
                         dst_ref=part,
                         send_sem=gain_sends.at[step - 1],
                         recv_sem=gain_recvs.at[step - 1],
@@ -216,33 +246,25 @@
 
             only(senders, start)
 
-    @pl.when(answerer)
+    merge_piece(kinds[1][0])
+    merge_piece(kinds[0][0])
+
+    @pl.when(hub)
+    def _():
+        pl.semaphore_wait(ready, len(targets))
+
+    @pl.when(jnp.logical_not(hub))
     def _():
         pl.semaphore_wait(barrier, len(targets))
-        for p in targets:
-            pl.semaphore_signal(ready, inc=1, device_id=p, device_id_type=MESH)
-
-    merge_piece(kinds[1][0])
-    merge_piece(kinds[0][0])
-
-    @pl.when(greeter)
-    def _():
-        pl.semaphore_wait(ready, len(targets))
+        for target, is_hub in zip(targets, nearby):
+            pl.when(is_hub)(functools.partial(greet, ready, target))
 
     step = 0
     for order, item in enumerate(in_turn(plan_of(kinds))):
         send(*item)
-        if order >= 24 and order % 18 == 6 and step <= len(gain_steps) + 1:
+        if order >= 24 and order % 16 == 8 and step <= len(gain_steps) + 1:
             pass_gains(step)
             step += 1
-
-    lane = lax.broadcasted_iota(jnp.int32, (1, 128), 1) // 32
-    for r in range(32):
-        first = r // 8 * 32 + r % 4 * 8 + r // 4 % 2
-        row = gains[first]
-        for k in range(1, 4):
-            row = jnp.where(lane == k, pltpu.roll(gains[first + 2 * k], 32 * k, 1), row)
-        out_norm[r : r + 1, :] = row
 
     for copies in sent:
         for copy in copies[-DEPTH:]:
@@ -261,7 +283,7 @@
         part = pl.ds(k * step, step)
         for m, (source, target) in enumerate(pairs):
             pltpu.make_async_copy(source.at[part], target.at[part], sems.at[m]).start()
-    out_gain[...] = gain[...].astype(jnp.bfloat16)
+    out_gain[...] = gain[...]
     for m, (source, target) in enumerate(pairs):
         pltpu.make_async_copy(source, target, sems.at[m]).wait()
 
@@ -277,7 +299,7 @@
         out_shape=(
             jax.ShapeDtypeStruct((width, whole), jnp.bfloat16),
             jax.ShapeDtypeStruct((width, whole), jnp.bfloat16),
-            jax.ShapeDtypeStruct((32, 128), jnp.float32),
+            jax.ShapeDtypeStruct((32, 128), jnp.bfloat16),
         ),
         in_specs=[hbm] * 8,
         out_specs=(vmem, vmem, vmem),
@@ -286,14 +308,14 @@
             pltpu.VMEM((2, rank, rows), jnp.bfloat16),
             pltpu.VMEM((2, rank, width), jnp.bfloat16),
             pltpu.VMEM((2, 1, 32), jnp.float32),
-            pltpu.VMEM((1, 1, 128), jnp.float32),
             pltpu.VMEM((128, 1, 128), jnp.float32),
+            pltpu.VMEM((32, 128), jnp.float32),
             pltpu.SemaphoreType.DMA((2, len(SPANS))),
             pltpu.SemaphoreType.DMA((3, 2)),
             pltpu.SemaphoreType.DMA((3, DEPTH)),
             pltpu.SemaphoreType.DMA((7, 2)),
-            pltpu.SemaphoreType.DMA((7,)),
-            pltpu.SemaphoreType.DMA((7,)),
+            pltpu.SemaphoreType.DMA((9,)),
+            pltpu.SemaphoreType.DMA((9,)),
             pltpu.SemaphoreType.REGULAR,
         ],
         compiler_params=pltpu.CompilerParams(

time: 106 us -> 104 us (0.981)
  Pallas kernels: 106 us -> 104 us
    pallas_call x1, Pallas kernels: 99.8 us -> 97.7 us  [per_device(): pl.pallas_call(kernel, out_shape=(jax.ShapeDtypeStruct((width, whole), jn...]
where the time goes in v4:
time: 104 us
  Pallas kernels  104 us (100%)
    pallas_call x1, Pallas kernels, per_device(): pl.pallas_call(kernel, out_shape=(jax.ShapeDtypeStruct((width, whole), jn...  97.7 us
    pallas_call x1, Pallas kernels, per_device(): pl.pallas_call(write_out, out_shape=(jax.ShapeDtypeStruct((width, whole),...  5.8 us

profile of v4, /device:TPU:0, one launch (start us, length us, event | category | flops | bytes accessed | tf_op | source)
XLA Modules:
  0.0 104.1 jit_solution(10810762623958159128)
XLA Ops:
  0.6 97.7 %shard_map.103 = (bf16[896,4096]{1,0:T(8,128)(2,1)S(1)}, bf16[896,4096]{1,0:T(8,128)(2,1)S(1)}, bf16[32,128]{1,0:T(8,128)(2,1)S(1)}) custom-call(bf16[512,896]{1,0:T(8,128)(2,1)} %train_gate.1, bf16[32,512]{1,0:T(8,128)(2,1)} %bitcast.5, bf16[32,896]{1,0:T(8,128)(2,1)} %high_gate.1, bf16[512,896]{1,0:T(8,128)(2,1)} %train_up.1, bf16[32,512]{1,0:T(8,128)(2,1)} %bitcast.6, ...), custom_call_target="tpu_custom_call" | custom-call | flops 1000000000 | bytes 20000000 | tf_op jit(solution)/shard_map/pallas_call | solution.py:297
  98.3 5.8 %shard_map.104 = (bf16[896,4096]{1,0:T(8,128)(2,1)}, bf16[896,4096]{1,0:T(8,128)(2,1)}, bf16[32,128]{1,0:T(8,128)(2,1)}) custom-call(bf16[896,4096]{1,0:T(8,128)(2,1)S(1)} %get-tuple-element.9.gate, bf16[896,4096]{1,0:T(8,128)(2,1)S(1)} %get-tuple-element.10.up, bf16[32,128]{1,0:T(8,128)(2,1)S(1)} %get-tuple-element.11.gain), custom_call_target="tpu_custom_call" | custom-call | flops 10000000 | bytes 30000000 | tf_op jit(solution)/shard_map/pallas_call | solution.py:334

commit v5 on v4

--- a/solution.py
+++ b/solution.py
@@ -18,7 +18,7 @@
 
 GROUP = 128
 CHUNK = 64
-SPANS = ((0, 1), (1, 2), (3, 4))
+SPANS = ((0, 1), (1, 6))
 PARTS = 7
 DEPTH = 4
 
@@ -101,36 +101,39 @@
         for p in peers:
             pl.semaphore_signal(sem, inc=1, device_id=p, device_id_type=MESH)
 
+    sources = ((train_gate, low_gate, high_gate), (train_up, low_up, high_up))
+    loads = {}
+
+    def load(m, s):
+        train, low, high = sources[m]
+        first, count = SPANS[s]
+        span = pl.ds(first * GROUP, count * GROUP)
+        started = [pltpu.make_async_copy(train.at[:, span], blocks.at[m, :, span], load_sems.at[m, s])]
+        if s == 0:
+            started.append(pltpu.make_async_copy(high, highs.at[m], small_sems.at[2 * m]))
+            started.append(pltpu.make_async_copy(low, lows.at[m], small_sems.at[2 * m + 1]))
+        for copy in started:
+            copy.start()
+        loads[m, first] = started
+
+    load(0, 0)
     for target, is_hub in zip(targets, nearby):
         pl.when(jnp.logical_not(is_hub))(functools.partial(greet, barrier, target))
     pl.when(hub)(functools.partial(greet, barrier, *other_hubs))
     pl.when(speaker)(functools.partial(greet, barrier, {"xh": 1, "c": 1}))
 
-    sources = ((train_gate, low_gate, high_gate), (train_up, low_up, high_up))
-    loads = {}
-    for s, (first, count) in enumerate(SPANS):
-        span = pl.ds(first * GROUP, count * GROUP)
-        for m, (train, low, high) in enumerate(sources):
-            if s == 0:
-                loads[m, "high"] = pltpu.make_async_copy(high, highs.at[m], small_sems.at[m, 0])
-                loads[m, "low"] = pltpu.make_async_copy(low, lows.at[m], small_sems.at[m, 1])
-                loads[m, "high"].start()
-                loads[m, "low"].start()
-            loads[m, first] = pltpu.make_async_copy(train.at[:, span], blocks.at[m, :, span], load_sems.at[m, s])
-            loads[m, first].start()
+    for m, s in ((1, 0), (0, 1), (1, 1)):
+        load(m, s)
     for k, norm in enumerate((norm_train, norm_step)):
-        pltpu.make_async_copy(norm, norms.at[k], small_sems.at[2, 0]).start()
+        pltpu.make_async_copy(norm, norms.at[k], small_sems.at[4]).start()
 
     def columns_of(owner):
         column = lax.rem(y + owner[0], 4) * 2 + (across_x if owner[1] else xl)
         return pl.ds(pl.multiple_of(column * rows, rows), rows)
 
     def merge(m, g):
-        if g == 0:
-            loads[m, "high"].wait()
-            loads[m, "low"].wait()
-        if (m, g) in loads:
-            loads[m, g].wait()
+        for copy in loads.get((m, g), ()):
+            copy.wait()
         span = pl.ds(g * GROUP, GROUP)
         high = highs[m, :, span].astype(jnp.float32).T.astype(jnp.bfloat16)
         product = jnp.dot(high, lows[m], preferred_element_type=jnp.float32)
@@ -216,7 +219,7 @@
 
     def pass_gains(step):
         if step == 0:
-            pltpu.make_async_copy(norms, norms, small_sems.at[2, 0]).wait()
+            pltpu.make_async_copy(norms, norms, small_sems.at[4]).wait()
             gains[me] = jnp.zeros((1, 128), jnp.float32)
             gains[me, :, 0:32] = norms[0] + norms[1]
             only(hub, meet)
@@ -224,7 +227,7 @@
         if step > 1:
             senders, part, peers, receivers, received = gain_steps[step - 2]
             count = 16 if part is out_norm else part.shape[0]
-            only(senders, functools.partial(settle, gain_sends.at[step - 2], count * len(peers)))
+            only(senders, functools.partial(settle, gain_sends.at[0], count * len(peers)))
             only(receivers, functools.partial(settle, gain_recvs.at[step - 2], received))
         if step <= len(gain_steps):
             senders, part, peers, _, _ = gain_steps[step - 1]
@@ -238,7 +241,7 @@
                     pltpu.make_async_remote_copy(
                         src_ref=part,
                         dst_ref=part,
-                        send_sem=gain_sends.at[step - 1],
+                        send_sem=gain_sends.at[0],
                         recv_sem=gain_recvs.at[step - 1],
                         device_id=p,
                         device_id_type=MESH,
@@ -283,9 +286,11 @@
         part = pl.ds(k * step, step)
         for m, (source, target) in enumerate(pairs):
             pltpu.make_async_copy(source.at[part], target.at[part], sems.at[m]).start()
-    out_gain[...] = gain[...]
+    small = pltpu.make_async_copy(gain, out_gain, sems.at[2])
+    small.start()
     for m, (source, target) in enumerate(pairs):
         pltpu.make_async_copy(source, target, sems.at[m]).wait()
+    small.wait()
 
 
 def per_device(train_gate, low_gate, high_gate, train_up, low_up, high_up, norm_train, norm_step):
@@ -311,10 +316,10 @@
             pltpu.VMEM((128, 1, 128), jnp.float32),
             pltpu.VMEM((32, 128), jnp.float32),
             pltpu.SemaphoreType.DMA((2, len(SPANS))),
-            pltpu.SemaphoreType.DMA((3, 2)),
+            pltpu.SemaphoreType.DMA((5,)),
             pltpu.SemaphoreType.DMA((3, DEPTH)),
             pltpu.SemaphoreType.DMA((7, 2)),
-            pltpu.SemaphoreType.DMA((9,)),
+            pltpu.SemaphoreType.DMA((1,)),
             pltpu.SemaphoreType.DMA((9,)),
             pltpu.SemaphoreType.REGULAR,
         ],
@@ -339,8 +344,8 @@
             jax.ShapeDtypeStruct((32, 128), jnp.bfloat16),
         ),
         in_specs=[vmem] * 3,
-        out_specs=(hbm, hbm, vmem),
-        scratch_shapes=[pltpu.SemaphoreType.DMA((2,))],
+        out_specs=(hbm, hbm, hbm),
+        scratch_shapes=[pltpu.SemaphoreType.DMA((3,))],
         compiler_params=pltpu.CompilerParams(vmem_limit_bytes=24 * 1024 * 1024),
         cost_estimate=pl.CostEstimate(flops=10**7, bytes_accessed=3 * 10**7, transcendentals=0),
     )(*gathered)

time: 104 us -> 104 us (level)
  no operation moved by 1% of the time
where the time goes in v5:
time: 104 us; the launch traced here: 103 us
  Pallas kernels  103 us (99%)
    pallas_call x1, Pallas kernels, per_device(): pl.pallas_call(kernel, out_shape=(jax.ShapeDtypeStruct((width, whole), jn...  97.6 us
    pallas_call x1, Pallas kernels, per_device(): pl.pallas_call(write_out, out_shape=(jax.ShapeDtypeStruct((width, whole),...  5.22 us

profile of v5, /device:TPU:0, one launch (start us, length us, event | category | flops | bytes accessed | tf_op | source)
XLA Modules:
  0.0 103.5 jit_solution(3476440681988255204)
XLA Ops:
  0.6 97.6 %shard_map.103 = (bf16[896,4096]{1,0:T(8,128)(2,1)S(1)}, bf16[896,4096]{1,0:T(8,128)(2,1)S(1)}, bf16[32,128]{1,0:T(8,128)(2,1)S(1)}) custom-call(bf16[512,896]{1,0:T(8,128)(2,1)} %train_gate.1, bf16[32,512]{1,0:T(8,128)(2,1)} %bitcast.5, bf16[32,896]{1,0:T(8,128)(2,1)} %high_gate.1, bf16[512,896]{1,0:T(8,128)(2,1)} %train_up.1, bf16[32,512]{1,0:T(8,128)(2,1)} %bitcast.6, ...), custom_call_target="tpu_custom_call" | custom-call | flops 1000000000 | bytes 20000000 | tf_op jit(solution)/shard_map/pallas_call | solution.py:302
  98.2 5.2 %shard_map.104 = (bf16[896,4096]{1,0:T(8,128)(2,1)}, bf16[896,4096]{1,0:T(8,128)(2,1)}, bf16[32,128]{1,0:T(8,128)(2,1)}) custom-call(bf16[896,4096]{1,0:T(8,128)(2,1)S(1)} %get-tuple-element.9.gate, bf16[896,4096]{1,0:T(8,128)(2,1)S(1)} %get-tuple-element.10.up, bf16[32,128]{1,0:T(8,128)(2,1)S(1)} %get-tuple-element.11.gain), custom_call_target="tpu_custom_call" | custom-call | flops 10000000 | bytes 30000000 | tf_op jit(solution)/shard_map/pallas_call | solution.py:339

commit v6 on v5

v6 whole, which is shorter than its diff:
```python
import functools

import jax
import jax.numpy as jnp
from jax import lax
from jax.experimental import pallas as pl
from jax.experimental.pallas import tpu as pltpu
from jax.sharding import Mesh
from jax.sharding import PartitionSpec as P

MESH = pl.DeviceIdType.MESH
AXES = ("y", "xl", "z", "xh", "c")
SHARD = ("y", "xl")
COLS = ("z", "xh", "c")
SIZES = (4, 2, 4, 2, 2)

mix_rate = 1.0

GROUP = 128
CHUNK = 64
PARTS = 4
DEPTH = 4
FIRST = (9, 12)
GAIN_EVERY = 8

OWN, BACK, AHEAD, FAR = (0, 0), (3, 0), (1, 0), (2, 0)


def shares_of(groups):
    every = [(m, g) for g in range(groups) for m in range(2)]
    return [(every[:count], every[count:]) for count in FIRST]


def chunks_of(share):
    pieces = [(m, g * GROUP + k, CHUNK) for m, g in share for k in range(0, GROUP, CHUNK)]
    kinds = ([], [])
    for k, piece in enumerate(pieces):
        kinds[0 if (k * 5) % 9 < 5 else 1].append(piece)
    excess = sum(piece[2] for piece in kinds[0]) - (len(share) * GROUP * 5 + 72) // 144 * 16
    if excess:
        giver, taker = kinds if excess > 0 else kinds[::-1]
        m, row, rows = giver.pop()
        giver.append((m, row, rows - abs(excess)))
        taker.append((m, row + rows - abs(excess), abs(excess)))
    return kinds


def plan_of(kinds):
    first, second = kinds
    up, down, across = [], [], []

    def add(link, held, seen, kind, pieces):
        link.extend((held, seen, kind, piece) for piece in pieces)

    for kind in (1, 0):
        add(up, OWN, BACK, kind, kinds[kind])
        add(down, OWN, AHEAD, kind, kinds[kind])
    add(up, BACK, FAR, 1, second[0::2])
    add(down, AHEAD, FAR, 1, second[1::2])
    add(up, (0, 1), (3, 1), 0, first)
    add(down, (0, 1), (1, 1), 0, first)
    add(up, BACK, FAR, 0, first[0::2])
    add(down, AHEAD, FAR, 0, first[1::2])
    add(up, (3, 1), (2, 1), 0, first[1::2])
    add(down, (1, 1), (2, 1), 0, first[0::2])
    add(across, OWN, (0, 1), 0, first)
    for held in (OWN, BACK, AHEAD, FAR):
        add(across, held, (held[0], 1), 1, second)
    return up, down, across


def in_turn(links):
    places, loads = [0] * len(links), [0] * len(links)
    while any(place < len(link) for place, link in zip(places, links)):
        k = min((loads[k], k) for k in range(len(links)) if places[k] < len(links[k]))[1]
        item = links[k][places[k]]
        yield (k, *item)
        places[k] += 1
        loads[k] += item[-1][2]


def greet(sem, *peers):
    for p in peers:
        pl.semaphore_signal(sem, inc=1, device_id=p, device_id_type=MESH)


def only(condition, act):
    if condition is None:
        act()
    else:
        pl.when(condition)(act)


def pass_rows(shares, sources, window, blocks, lows, highs, load_sems, small_sems, send_sems, recv_sems, enter, between):
    y, xl, c = (lax.axis_index(name) for name in ("y", "xl", "c"))
    rows = sources[0][0].shape[0]
    across_x = 1 - xl
    targets = ({"y": lax.rem(y + 1, 4)}, {"y": lax.rem(y + 3, 4)}, {"xl": across_x})

    def columns_of(owner):
        column = lax.rem(y + owner[0], 4) * 2 + (across_x if owner[1] else xl)
        return pl.ds(pl.multiple_of(column * rows, rows), rows)

    def run(core, share):
        loads = {}

        def load(m, groups, sem, small):
            train, low, high = sources[m]
            span = pl.ds(groups[0] * GROUP, len(groups) * GROUP)
            started = [pltpu.make_async_copy(train.at[:, span], blocks.at[m, :, span], load_sems.at[m, sem])]
            if small:
                started.append(pltpu.make_async_copy(high, highs.at[m], small_sems.at[2 * m]))
                started.append(pltpu.make_async_copy(low, lows.at[m], small_sems.at[2 * m + 1]))
            for copy in started:
                copy.start()
            loads[m, groups[0]] = started

        mine = [[g for m, g in share if m == k] for k in range(2)]
        order = (share[0][0], 1 - share[0][0])
        for m in order:
            if mine[m]:
                load(m, mine[m][:1], 0, True)
        for m in order:
            if mine[m][1:]:
                load(m, mine[m][1:], 1, False)

        def merge(m, g):
            for copy in loads.get((m, g), ()):
                copy.wait()
            span = pl.ds(g * GROUP, GROUP)
            high = highs[m, :, span].astype(jnp.float32).T.astype(jnp.bfloat16)
            product = jnp.dot(high, lows[m], preferred_element_type=jnp.float32)
            latest = blocks[m, :, span].T.astype(jnp.float32) + mix_rate * product
            ref, row = window(share, m, g * GROUP)
            ref[pl.ds(row, GROUP), columns_of(OWN)] = latest.astype(jnp.bfloat16)

        kinds = chunks_of(share)
        totals = [sum(piece[2] for piece in pieces) for pieces in kinds]
        merged, arrived = set(), set()
        sent = ([], [], [])

        def merge_piece(piece):
            at = (piece[0], piece[1] // GROUP)
            if at not in merged:
                merged.add(at)
                merge(*at)

        def receive(owner, kind):
            if (owner, kind) not in arrived:
                arrived.add((owner, kind))
                as_many = window(share, share[0][0], share[0][1] * GROUP)[0].at[pl.ds(0, totals[kind] // 2), pl.ds(0, 2 * rows)]
                sem = recv_sems.at[owner[0] * 2 + owner[1] - 1, kind]
                pltpu.make_async_copy(as_many, as_many, sem).wait()

        def send(link, held, seen, kind, piece):
            order = len(sent[link])
            if order >= DEPTH:
                sent[link][order - DEPTH].wait_send()
            if held == OWN:
                merge_piece(piece)
            else:
                receive(held, kind)
            m, row, count = piece
            ref, row = window(share, m, row)
            part = ref.at[pl.ds(row, count), columns_of(held)]
            copy = pltpu.make_async_remote_copy(
                src_ref=part,
                dst_ref=part,
                send_sem=send_sems.at[link, order % DEPTH],
                recv_sem=recv_sems.at[seen[0] * 2 + seen[1] - 1, kind],
                device_id=targets[link],
                device_id_type=MESH,
            )
            copy.start()
            sent[link].append(copy)

        merge_piece(kinds[1][0])
        merge_piece(kinds[0][0])
        enter(targets)
        for order, item in enumerate(in_turn(plan_of(kinds))):
            send(*item)
            between(order)
        for copies in sent:
            for copy in copies[-DEPTH:]:
                copy.wait_send()
        for oy in range(4):
            for ox in range(2):
                if (oy, ox) != OWN:
                    receive((oy, ox), 0)
                    receive((oy, ox), 1)

    for core, share in enumerate(shares):
        pl.when(c == core)(functools.partial(run, core, share))


def first_kernel(
    train_gate, low_gate, high_gate, train_up, low_up, high_up, norm_train, norm_step,
    out_gate, out_up, out_norm,
    blocks, lows, highs, load_sems, small_sems, send_sems, recv_sems,
    norms, gains, packed, gain_sends, gain_recvs, ready,
):
    y, xl, z, xh, c = (lax.axis_index(name) for name in AXES)
    y_next, y_last = lax.rem(y + 1, 4), lax.rem(y + 3, 4)
    across_x = 1 - xl
    targets = ({"y": y_next}, {"y": y_last}, {"xl": across_x})
    neighbours = ((y_next, xl), (y_last, xl), (y, across_x))

    def at_gate(yy, xx):
        return jnp.logical_and(yy == 1, xx == 0)

    hub_group = jnp.logical_and(xh == 1, c == 1)
    gate = at_gate(y, xl)
    hub = jnp.logical_and(gate, hub_group)
    speaker = jnp.logical_and(gate, jnp.logical_not(hub_group))
    nearby = [jnp.logical_and(hub_group, at_gate(*place)) for place in neighbours]
    other_hubs = [{"z": lax.rem(z + k, 4)} for k in (1, 3, 2)]
    speakers = [{"c": 0}, {"xh": 0}, {"xh": 0, "c": 0}]
    barrier = pltpu.get_barrier_semaphore()

    for target, is_hub in zip(targets, nearby):
        pl.when(jnp.logical_not(is_hub))(functools.partial(greet, barrier, target))
    pl.when(hub)(functools.partial(greet, barrier, *other_hubs))
    pl.when(speaker)(functools.partial(greet, barrier, {"xh": 1, "c": 1}))
    for k, norm in enumerate((norm_train, norm_step)):
        pltpu.make_async_copy(norm, norms.at[k], small_sems.at[4]).start()

    def enter(targets):
        @pl.when(hub)
        def _():
            pl.semaphore_wait(ready, len(targets))

        @pl.when(jnp.logical_not(hub))
        def _():
            pl.semaphore_wait(barrier, len(targets))
            for target, is_hub in zip(targets, nearby):
                pl.when(is_hub)(functools.partial(greet, ready, target))

    col = (z * 2 + xh) * 2 + c
    me = col * 8 + y * 2 + xl
    gain_steps = (
        (None, gains.at[pl.ds(me, 1)], targets[2:], None, 1),
        (None, gains.at[pl.ds(me // 2 * 2, 2)], targets[:2], None, 4),
        (None, gains.at[pl.ds(col * 8 + y_last * 2, 2)], targets[:1], None, 2),
        (speaker, gains.at[pl.ds(col * 8, 8)], [{"xh": 1, "c": 1}], hub, 24),
        (hub, gains.at[pl.ds(z * 32, 32)], other_hubs, hub, 96),
        (hub, out_norm, speakers, speaker, 16),
        (gate, out_norm, targets[2:], jnp.logical_and(y == 1, xl == 1), 16),
        (y == 1, out_norm, targets[:2], jnp.logical_or(y == 0, y == 2), 16),
        (y == 2, out_norm, targets[:1], y == 3, 16),
    )

    def settle(sem, count):
        as_many = gains.at[pl.ds(0, count)]
        pltpu.make_async_copy(as_many, as_many, sem).wait()

    def pack():
        lane = lax.broadcasted_iota(jnp.int32, (1, 128), 1) // 32
        for r in range(32):
            first = r % 4 * 32 + r // 4
            row = gains[first]
            for k in range(1, 4):
                row = jnp.where(lane == k, pltpu.roll(gains[first + 8 * k], 32 * k, 1), row)
            packed[r : r + 1, :] = row
        out_norm[...] = packed[...].astype(jnp.bfloat16)

    def meet():
        pl.semaphore_wait(barrier, len(other_hubs) + len(speakers))
        greet(ready, *speakers)

    def pass_gains(step):
        if step == 0:
            pltpu.make_async_copy(norms, norms, small_sems.at[4]).wait()
            gains[me] = jnp.zeros((1, 128), jnp.float32)
            gains[me, :, 0:32] = norms[0] + norms[1]
            only(hub, meet)
            return
        if step > 1:
            senders, part, peers, receivers, received = gain_steps[step - 2]
            count = 16 if part is out_norm else part.shape[0]
            only(senders, functools.partial(settle, gain_sends.at[0], count * len(peers)))
            only(receivers, functools.partial(settle, gain_recvs.at[step - 2], received))
        if step <= len(gain_steps):
            senders, part, peers, _, _ = gain_steps[step - 1]

            def start():
                if step == 4:
                    pl.semaphore_wait(ready, 1)
                if step == 6:
                    pack()
                for p in peers:
                    pltpu.make_async_remote_copy(
                        src_ref=part,
                        dst_ref=part,
                        send_sem=gain_sends.at[0],
                        recv_sem=gain_recvs.at[step - 1],
                        device_id=p,
                        device_id_type=MESH,
                    ).start()

            only(senders, start)

    def between(order):
        step, rest = divmod(order - 24, GAIN_EVERY)
        if step >= 0 and rest == 0 and step <= len(gain_steps) + 1:
            pass_gains(step)

    outs = (out_gate, out_up)
    pass_rows(
        [first for first, _ in shares_of(train_gate.shape[1] // GROUP)],
        ((train_gate, low_gate, high_gate), (train_up, low_up, high_up)),
        lambda share, m, row: (outs[m], row),
        blocks, lows, highs, load_sems, small_sems, send_sems, recv_sems, enter, between,
    )


def second_kernel(
    train_gate, low_gate, high_gate, train_up, low_up, high_up, after,
    out,
    blocks, lows, highs, load_sems, small_sems, send_sems, recv_sems,
):
    y, xl = lax.axis_index("y"), lax.axis_index("xl")
    barrier = pltpu.get_barrier_semaphore()
    greet(barrier, {"y": lax.rem(y + 1, 4)}, {"y": lax.rem(y + 3, 4)}, {"xl": 1 - xl})
    pass_rows(
        [second for _, second in shares_of(train_gate.shape[1] // GROUP)],
        ((train_gate, low_gate, high_gate), (train_up, low_up, high_up)),
        lambda share, m, row: (out, share.index((m, row // GROUP)) * GROUP + row % GROUP),
        blocks, lows, highs, load_sems, small_sems, send_sems, recv_sems,
        lambda targets: pl.semaphore_wait(barrier, len(targets)),
        lambda order: None,
    )


def write_first(gate, up, gain, out_gate, out_up, out_gain, sems):
    shares = shares_of(gate.shape[0] // GROUP)
    small = pltpu.make_async_copy(gain, out_gain, sems.at[2])
    small.start()

    def run(share):
        pairs = ((gate, out_gate), (up, out_up))
        ends = [GROUP * sum(m == k for m, _ in share) for k in range(2)]
        for k in range(PARTS):
            for m, (source, target) in enumerate(pairs):
                first, last = (ends[m] // GROUP * n // PARTS * GROUP for n in (k, k + 1))
                if last > first:
                    part = pl.ds(first, last - first)
                    pltpu.make_async_copy(source.at[part], target.at[part], sems.at[m]).start()
        for m, (source, target) in enumerate(pairs):
            part = pl.ds(0, ends[m])
            pltpu.make_async_copy(source.at[part], target.at[part], sems.at[m]).wait()

    for core, (share, _) in enumerate(shares):
        pl.when(lax.axis_index("c") == core)(functools.partial(run, share))
    small.wait()


def write_second(rest, held_gate, held_up, out_gate, out_up, sems):
    shares = shares_of(out_gate.shape[0] // GROUP)

    def run(share):
        copies = []
        for k, (m, g) in enumerate(share):
            source = rest.at[pl.ds(k * GROUP, GROUP)]
            target = (out_gate, out_up)[m].at[pl.ds(g * GROUP, GROUP)]
            copies.append(pltpu.make_async_copy(source, target, sems.at[k]))
            copies[-1].start()
        for copy in copies:
            copy.wait()

    for core, (_, share) in enumerate(shares):
        pl.when(lax.axis_index("c") == core)(functools.partial(run, share))


def per_device(train_gate, low_gate, high_gate, train_up, low_up, high_up, norm_train, norm_step):
    rows, width = train_gate.shape
    whole = rows * 8
    rank = low_gate.shape[1]
    most = max(2 * width // GROUP - count for count in FIRST)
    vmem = pl.BlockSpec(memory_space=pltpu.VMEM)
    hbm = pl.BlockSpec(memory_space=pltpu.HBM)
    matrix = jax.ShapeDtypeStruct((width, whole), jnp.bfloat16)
    gain = jax.ShapeDtypeStruct((32, 128), jnp.bfloat16)
    sources = [
        pltpu.with_memory_space_constraint(x, pltpu.HBM)
        for x in (
            train_gate, low_gate.T, high_gate, train_up, low_up.T, high_up,
            norm_train.reshape(1, 32), norm_step.reshape(1, 32),
        )
    ]
    scratch = [
        pltpu.VMEM((2, rows, width), jnp.bfloat16),
        pltpu.VMEM((2, rank, rows), jnp.bfloat16),
        pltpu.VMEM((2, rank, width), jnp.bfloat16),
        pltpu.SemaphoreType.DMA((2, 2)),
        pltpu.SemaphoreType.DMA((5,)),
        pltpu.SemaphoreType.DMA((3, DEPTH)),
        pltpu.SemaphoreType.DMA((7, 2)),
    ]
    limit = 12 * 1024 * 1024
    gathered = pl.pallas_call(
        first_kernel,
        out_shape=(matrix, matrix, gain),
        in_specs=[hbm] * 8,
        out_specs=(vmem, vmem, vmem),
        scratch_shapes=scratch
        + [
            pltpu.VMEM((2, 1, 32), jnp.float32),
            pltpu.VMEM((128, 1, 128), jnp.float32),
            pltpu.VMEM((32, 128), jnp.float32),
            pltpu.SemaphoreType.DMA((1,)),
            pltpu.SemaphoreType.DMA((9,)),
            pltpu.SemaphoreType.REGULAR,
        ],
        compiler_params=pltpu.CompilerParams(collective_id=0, has_side_effects=True, vmem_limit_bytes=limit),
        cost_estimate=pl.CostEstimate(flops=10**9, bytes_accessed=2 * 10**7, transcendentals=0),
    )(*sources)
    held_gate, held_up, served = pl.pallas_call(
        write_first,
        out_shape=(matrix, matrix, gain),
        in_specs=[vmem] * 3,
        out_specs=(hbm, hbm, hbm),
        scratch_shapes=[pltpu.SemaphoreType.DMA((3,))],
        compiler_params=pltpu.CompilerParams(vmem_limit_bytes=limit),
        cost_estimate=pl.CostEstimate(flops=10**7, bytes_accessed=3 * 10**7, transcendentals=0),
    )(*gathered)
    rest = pl.pallas_call(
        second_kernel,
        out_shape=jax.ShapeDtypeStruct((most * GROUP, whole), jnp.bfloat16),
        in_specs=[hbm] * 7,
        out_specs=vmem,
        scratch_shapes=scratch,
        compiler_params=pltpu.CompilerParams(collective_id=1, has_side_effects=True, vmem_limit_bytes=limit),
        cost_estimate=pl.CostEstimate(flops=10**9, bytes_accessed=2 * 10**7, transcendentals=0),
    )(*sources[:6], pltpu.with_memory_space_constraint(served, pltpu.HBM))
    ready_gate, ready_up = pl.pallas_call(
        write_second,
        out_shape=(matrix, matrix),
        in_specs=[vmem, hbm, hbm],
        out_specs=(hbm, hbm),
        input_output_aliases={1: 0, 2: 1},
        scratch_shapes=[pltpu.SemaphoreType.DMA((most,))],
        compiler_params=pltpu.CompilerParams(vmem_limit_bytes=limit),
        cost_estimate=pl.CostEstimate(flops=10**7, bytes_accessed=10**7, transcendentals=0),
    )(rest, held_gate, held_up)
    return (ready_gate, ready_up, served.reshape(-1))


def solution(mesh):
    finer = Mesh(mesh.devices.reshape(SIZES), AXES)
    placed = (
        P(SHARD, COLS),
        P(SHARD, None),
        P(None, COLS),
        P(SHARD, COLS),
        P(SHARD, None),
        P(None, COLS),
        P(SHARD + COLS),
        P(SHARD + COLS),
    )
    return jax.shard_map(
        per_device,
        mesh=finer,
        in_specs=placed,
        out_specs=(P(COLS, None), P(COLS, None), P()),
        check_vma=False,
    )
```

time: 104 us -> 101 us (0.971)
  Pallas kernels: 103 us -> 99.9 us
    pallas_call x2 -> x4, Pallas kernels: 103 us -> 99.9 us  [the longest x1 65.7 us: per_device(): pl.pallas_call(first_kernel, out_shape=(matrix, matrix, gain), in_specs=[...]
where the time goes in v6:
time: 101 us
  Pallas kernels  99.9 us (99%)
    pallas_call x1, Pallas kernels, per_device(): pl.pallas_call(first_kernel, out_shape=(matrix, matrix, gain), in_specs=[...  65.7 us
    pallas_call x1, Pallas kernels, per_device(): pl.pallas_call(second_kernel, out_shape=jax.ShapeDtypeStruct((most * GROU...  28.2 us
    pallas_call x1, Pallas kernels, per_device(): pl.pallas_call(write_first, out_shape=(matrix, matrix, gain), in_specs=[v...  3.65 us
    pallas_call x1, Pallas kernels, per_device(): pl.pallas_call(write_second, out_shape=(matrix, matrix), in_specs=[vmem,...  2.4 us

profile of v6, /device:TPU:0, one launch (start us, length us, event | category | flops | bytes accessed | tf_op | source)
XLA Modules:
  0.0 100.6 jit_solution(231940988569515879)
XLA Ops:
  0.6 65.7 %shard_map.103 = (bf16[896,4096]{1,0:T(8,128)(2,1)S(1)}, bf16[896,4096]{1,0:T(8,128)(2,1)S(1)}, bf16[32,128]{1,0:T(8,128)(2,1)S(1)}) custom-call(bf16[512,896]{1,0:T(8,128)(2,1)} %train_gate.3, bf16[32,512]{1,0:T(8,128)(2,1)} %bitcast.5, bf16[32,896]{1,0:T(8,128)(2,1)} %high_gate.3, bf16[512,896]{1,0:T(8,128)(2,1)} %train_up.3, bf16[32,512]{1,0:T(8,128)(2,1)} %bitcast.7, ...), custom_call_target="tpu_custom_call" | custom-call | flops 1000000000 | bytes 20000000 | tf_op jit(solution)/shard_map/pallas_call | solution.py:400
  66.4 3.6 %shard_map.104 = (bf16[896,4096]{1,0:T(8,128)(2,1)}, bf16[896,4096]{1,0:T(8,128)(2,1)}, bf16[32,128]{1,0:T(8,128)(2,1)}) custom-call(bf16[896,4096]{1,0:T(8,128)(2,1)S(1)} %get-tuple-element.11.gate, bf16[896,4096]{1,0:T(8,128)(2,1)S(1)} %get-tuple-element.12.up, bf16[32,128]{1,0:T(8,128)(2,1)S(1)} %get-tuple-element.13.gain), custom_call_target="tpu_custom_call" | custom-call | flops 10000000 | bytes 30000000 | tf_op jit(solution)/shard_map/pallas_call | solution.py:417
  70.0 28.2 %shard_map.105.rest = bf16[640,4096]{1,0:T(8,128)(2,1)S(1)} custom-call(bf16[512,896]{1,0:T(8,128)(2,1)} %train_gate.3, bf16[32,512]{1,0:T(8,128)(2,1)} %bitcast.6, bf16[32,896]{1,0:T(8,128)(2,1)} %high_gate.3, bf16[512,896]{1,0:T(8,128)(2,1)} %train_up.3, bf16[32,512]{1,0:T(8,128)(2,1)} %bitcast.8, bf16[32,896]{1,0:T(8,128)(2,1)} %high_up.3, ...), custom_call_target="tpu_custom_call" | custom-call | flops 1000000000 | bytes 20000000 | tf_op jit(solution)/shard_map/pallas_call | solution.py:426
  98.2 2.4 %shard_map.106 = (bf16[896,4096]{1,0:T(8,128)(2,1)}, bf16[896,4096]{1,0:T(8,128)(2,1)}) custom-call(bf16[640,4096]{1,0:T(8,128)(2,1)S(1)} %shard_map.105.rest, bf16[896,4096]{1,0:T(8,128)(2,1)} %get-tuple-element.15.held_gate, bf16[896,4096]{1,0:T(8,128)(2,1)} %get-tuple-element.16.held_up), custom_call_target="tpu_custom_call", output_to_operand_aliasing={{0}: (1, {}), {1}: (2, {})} | custom-call | flops 10000000 | bytes 10000000 | tf_op jit(solution)/shard_map/pallas_call | solution.py:435

commit v7 on v6

--- a/solution.py
+++ b/solution.py
@@ -19,7 +19,7 @@
 GROUP = 128
 CHUNK = 64
 PARTS = 4
-DEPTH = 4
+DEPTH = 6
 FIRST = (9, 12)
 GAIN_EVERY = 8
 
@@ -144,6 +144,11 @@
             if at not in merged:
                 merged.add(at)
                 merge(*at)
+
+        def merge_next():
+            at = next(at for at in share if at not in merged)
+            merged.add(at)
+            merge(*at)
 
         def receive(owner, kind):
             if (owner, kind) not in arrived:
@@ -179,6 +184,8 @@
         enter(targets)
         for order, item in enumerate(in_turn(plan_of(kinds))):
             send(*item)
+            if order % 3 == 2 and len(merged) < len(share):
+                merge_next()
             between(order)
         for copies in sent:
             for copy in copies[-DEPTH:]:

time: 101 us -> 101 us (level)
  no operation moved by 1% of the time
where the time goes in v7:
time: 101 us
  Pallas kernels  100 us (99%)
    pallas_call x1, Pallas kernels, per_device(): pl.pallas_call(first_kernel, out_shape=(matrix, matrix, gain), in_specs=[...  65.8 us
    pallas_call x1, Pallas kernels, per_device(): pl.pallas_call(second_kernel, out_shape=jax.ShapeDtypeStruct((most * GROU...  28.2 us
    pallas_call x1, Pallas kernels, per_device(): pl.pallas_call(write_first, out_shape=(matrix, matrix, gain), in_specs=[v...  3.65 us
    pallas_call x1, Pallas kernels, per_device(): pl.pallas_call(write_second, out_shape=(matrix, matrix), in_specs=[vmem,...  2.4 us

profile of v7, /device:TPU:0, one launch (start us, length us, event | category | flops | bytes accessed | tf_op | source)
XLA Modules:
  0.0 100.7 jit_solution(16432639939941787135)
XLA Ops:
  0.6 65.8 %shard_map.103 = (bf16[896,4096]{1,0:T(8,128)(2,1)S(1)}, bf16[896,4096]{1,0:T(8,128)(2,1)S(1)}, bf16[32,128]{1,0:T(8,128)(2,1)S(1)}) custom-call(bf16[512,896]{1,0:T(8,128)(2,1)} %train_gate.3, bf16[32,512]{1,0:T(8,128)(2,1)} %bitcast.5, bf16[32,896]{1,0:T(8,128)(2,1)} %high_gate.3, bf16[512,896]{1,0:T(8,128)(2,1)} %train_up.3, bf16[32,512]{1,0:T(8,128)(2,1)} %bitcast.7, ...), custom_call_target="tpu_custom_call" | custom-call | flops 1000000000 | bytes 20000000 | tf_op jit(solution)/shard_map/pallas_call | solution.py:407
  66.4 3.6 %shard_map.104 = (bf16[896,4096]{1,0:T(8,128)(2,1)}, bf16[896,4096]{1,0:T(8,128)(2,1)}, bf16[32,128]{1,0:T(8,128)(2,1)}) custom-call(bf16[896,4096]{1,0:T(8,128)(2,1)S(1)} %get-tuple-element.11.gate, bf16[896,4096]{1,0:T(8,128)(2,1)S(1)} %get-tuple-element.12.up, bf16[32,128]{1,0:T(8,128)(2,1)S(1)} %get-tuple-element.13.gain), custom_call_target="tpu_custom_call" | custom-call | flops 10000000 | bytes 30000000 | tf_op jit(solution)/shard_map/pallas_call | solution.py:424
  70.1 28.2 %shard_map.105.rest = bf16[640,4096]{1,0:T(8,128)(2,1)S(1)} custom-call(bf16[512,896]{1,0:T(8,128)(2,1)} %train_gate.3, bf16[32,512]{1,0:T(8,128)(2,1)} %bitcast.6, bf16[32,896]{1,0:T(8,128)(2,1)} %high_gate.3, bf16[512,896]{1,0:T(8,128)(2,1)} %train_up.3, bf16[32,512]{1,0:T(8,128)(2,1)} %bitcast.8, bf16[32,896]{1,0:T(8,128)(2,1)} %high_up.3, ...), custom_call_target="tpu_custom_call" | custom-call | flops 1000000000 | bytes 20000000 | tf_op jit(solution)/shard_map/pallas_call | solution.py:433
  98.3 2.4 %shard_map.106 = (bf16[896,4096]{1,0:T(8,128)(2,1)}, bf16[896,4096]{1,0:T(8,128)(2,1)}) custom-call(bf16[640,4096]{1,0:T(8,128)(2,1)S(1)} %shard_map.105.rest, bf16[896,4096]{1,0:T(8,128)(2,1)} %get-tuple-element.15.held_gate, bf16[896,4096]{1,0:T(8,128)(2,1)} %get-tuple-element.16.held_up), custom_call_target="tpu_custom_call", output_to_operand_aliasing={{0}: (1, {}), {1}: (2, {})} | custom-call | flops 10000000 | bytes 10000000 | tf_op jit(solution)/shard_map/pallas_call | solution.py:442

commit v8 on v6

--- a/solution.py
+++ b/solution.py
@@ -45,7 +45,7 @@
     return kinds
 
 
-def plan_of(kinds):
+def plan_of(kinds, partners_first):
     first, second = kinds
     up, down, across = [], [], []
 
@@ -55,10 +55,13 @@
     for kind in (1, 0):
         add(up, OWN, BACK, kind, kinds[kind])
         add(down, OWN, AHEAD, kind, kinds[kind])
-    add(up, BACK, FAR, 1, second[0::2])
-    add(down, AHEAD, FAR, 1, second[1::2])
-    add(up, (0, 1), (3, 1), 0, first)
-    add(down, (0, 1), (1, 1), 0, first)
+    for partners in (partners_first, not partners_first):
+        if partners:
+            add(up, (0, 1), (3, 1), 0, first)
+            add(down, (0, 1), (1, 1), 0, first)
+        else:
+            add(up, BACK, FAR, 1, second[0::2])
+            add(down, AHEAD, FAR, 1, second[1::2])
     add(up, BACK, FAR, 0, first[0::2])
     add(down, AHEAD, FAR, 0, first[1::2])
     add(up, (3, 1), (2, 1), 0, first[1::2])
@@ -91,7 +94,7 @@
         pl.when(condition)(act)
 
 
-def pass_rows(shares, sources, window, blocks, lows, highs, load_sems, small_sems, send_sems, recv_sems, enter, between):
+def pass_rows(partners_first, shares, sources, window, blocks, lows, highs, load_sems, small_sems, send_sems, recv_sems, enter, between):
     y, xl, c = (lax.axis_index(name) for name in ("y", "xl", "c"))
     rows = sources[0][0].shape[0]
     across_x = 1 - xl
@@ -177,7 +180,7 @@
         merge_piece(kinds[1][0])
         merge_piece(kinds[0][0])
         enter(targets)
-        for order, item in enumerate(in_turn(plan_of(kinds))):
+        for order, item in enumerate(in_turn(plan_of(kinds, partners_first))):
             send(*item)
             between(order)
         for copies in sent:
@@ -306,6 +309,7 @@
 
     outs = (out_gate, out_up)
     pass_rows(
+        False,
         [first for first, _ in shares_of(train_gate.shape[1] // GROUP)],
         ((train_gate, low_gate, high_gate), (train_up, low_up, high_up)),
         lambda share, m, row: (outs[m], row),
@@ -322,6 +326,7 @@
     barrier = pltpu.get_barrier_semaphore()
     greet(barrier, {"y": lax.rem(y + 1, 4)}, {"y": lax.rem(y + 3, 4)}, {"xl": 1 - xl})
     pass_rows(
+        True,
         [second for _, second in shares_of(train_gate.shape[1] // GROUP)],
         ((train_gate, low_gate, high_gate), (train_up, low_up, high_up)),
         lambda share, m, row: (out, share.index((m, row // GROUP)) * GROUP + row % GROUP),
@@ -358,14 +363,15 @@
     shares = shares_of(out_gate.shape[0] // GROUP)
 
     def run(share):
-        copies = []
+        half = GROUP // 2
         for k, (m, g) in enumerate(share):
-            source = rest.at[pl.ds(k * GROUP, GROUP)]
-            target = (out_gate, out_up)[m].at[pl.ds(g * GROUP, GROUP)]
-            copies.append(pltpu.make_async_copy(source, target, sems.at[k]))
-            copies[-1].start()
-        for copy in copies:
-            copy.wait()
+            for part in range(0, GROUP, half):
+                source = rest.at[pl.ds(k * GROUP + part, half)]
+                target = (out_gate, out_up)[m].at[pl.ds(g * GROUP + part, half)]
+                pltpu.make_async_copy(source, target, sems.at[0]).start()
+        whole = rest.at[pl.ds(0, len(share) * GROUP)]
+        target = out_gate.at[pl.ds(0, len(share) * GROUP)]
+        pltpu.make_async_copy(whole, target, sems.at[0]).wait()
 
     for core, (_, share) in enumerate(shares):
         pl.when(lax.axis_index("c") == core)(functools.partial(run, share))
@@ -438,7 +444,7 @@
         in_specs=[vmem, hbm, hbm],
         out_specs=(hbm, hbm),
         input_output_aliases={1: 0, 2: 1},
-        scratch_shapes=[pltpu.SemaphoreType.DMA((most,))],
+        scratch_shapes=[pltpu.SemaphoreType.DMA((1,))],
         compiler_params=pltpu.CompilerParams(vmem_limit_bytes=limit),
         cost_estimate=pl.CostEstimate(flops=10**7, bytes_accessed=10**7, transcendentals=0),
     )(rest, held_gate, held_up)

time: 101 us -> 101 us (level)
  no operation moved by 1% of the time
where the time goes in v8:
time: 101 us; the launch traced here: 99.9 us
  Pallas kernels  99.2 us (98%)
    pallas_call x1, Pallas kernels, per_device(): pl.pallas_call(first_kernel, out_shape=(matrix, matrix, gain), in_specs=[...  65.7 us
    pallas_call x1, Pallas kernels, per_device(): pl.pallas_call(second_kernel, out_shape=jax.ShapeDtypeStruct((most * GROU...  27.5 us
    pallas_call x1, Pallas kernels, per_device(): pl.pallas_call(write_first, out_shape=(matrix, matrix, gain), in_specs=[v...  3.65 us
    pallas_call x1, Pallas kernels, per_device(): pl.pallas_call(write_second, out_shape=(matrix, matrix), in_specs=[vmem,...  2.35 us

profile of v8, /device:TPU:0, one launch (start us, length us, event | category | flops | bytes accessed | tf_op | source)
XLA Modules:
  0.0 99.9 jit_solution(18008310166236702015)
XLA Ops:
  0.6 65.7 %shard_map.103 = (bf16[896,4096]{1,0:T(8,128)(2,1)S(1)}, bf16[896,4096]{1,0:T(8,128)(2,1)S(1)}, bf16[32,128]{1,0:T(8,128)(2,1)S(1)}) custom-call(bf16[512,896]{1,0:T(8,128)(2,1)} %train_gate.3, bf16[32,512]{1,0:T(8,128)(2,1)} %bitcast.5, bf16[32,896]{1,0:T(8,128)(2,1)} %high_gate.3, bf16[512,896]{1,0:T(8,128)(2,1)} %train_up.3, bf16[32,512]{1,0:T(8,128)(2,1)} %bitcast.7, ...), custom_call_target="tpu_custom_call" | custom-call | flops 1000000000 | bytes 20000000 | tf_op jit(solution)/shard_map/pallas_call | solution.py:406
  66.4 3.6 %shard_map.104 = (bf16[896,4096]{1,0:T(8,128)(2,1)}, bf16[896,4096]{1,0:T(8,128)(2,1)}, bf16[32,128]{1,0:T(8,128)(2,1)}) custom-call(bf16[896,4096]{1,0:T(8,128)(2,1)S(1)} %get-tuple-element.11.gate, bf16[896,4096]{1,0:T(8,128)(2,1)S(1)} %get-tuple-element.12.up, bf16[32,128]{1,0:T(8,128)(2,1)S(1)} %get-tuple-element.13.gain), custom_call_target="tpu_custom_call" | custom-call | flops 10000000 | bytes 30000000 | tf_op jit(solution)/shard_map/pallas_call | solution.py:423
  70.0 27.5 %shard_map.105.rest = bf16[640,4096]{1,0:T(8,128)(2,1)S(1)} custom-call(bf16[512,896]{1,0:T(8,128)(2,1)} %train_gate.3, bf16[32,512]{1,0:T(8,128)(2,1)} %bitcast.6, bf16[32,896]{1,0:T(8,128)(2,1)} %high_gate.3, bf16[512,896]{1,0:T(8,128)(2,1)} %train_up.3, bf16[32,512]{1,0:T(8,128)(2,1)} %bitcast.8, bf16[32,896]{1,0:T(8,128)(2,1)} %high_up.3, ...), custom_call_target="tpu_custom_call" | custom-call | flops 1000000000 | bytes 20000000 | tf_op jit(solution)/shard_map/pallas_call | solution.py:432
  97.5 2.3 %shard_map.106 = (bf16[896,4096]{1,0:T(8,128)(2,1)}, bf16[896,4096]{1,0:T(8,128)(2,1)}) custom-call(bf16[640,4096]{1,0:T(8,128)(2,1)S(1)} %shard_map.105.rest, bf16[896,4096]{1,0:T(8,128)(2,1)} %get-tuple-element.15.held_gate, bf16[896,4096]{1,0:T(8,128)(2,1)} %get-tuple-element.16.held_up), custom_call_target="tpu_custom_call", output_to_operand_aliasing={{0}: (1, {}), {1}: (2, {})} | custom-call | flops 10000000 | bytes 10000000 | tf_op jit(solution)/shard_map/pallas_call | solution.py:441

commit v9 on v6

--- a/solution.py
+++ b/solution.py
@@ -91,7 +91,7 @@
         pl.when(condition)(act)
 
 
-def pass_rows(shares, sources, window, blocks, lows, highs, load_sems, small_sems, send_sems, recv_sems, enter, between):
+def pass_rows(shares, sources, window, blocks, lows, highs, load_sems, small_sems, send_sems, recv_sems, begin, enter, between):
     y, xl, c = (lax.axis_index(name) for name in ("y", "xl", "c"))
     rows = sources[0][0].shape[0]
     across_x = 1 - xl
@@ -120,6 +120,8 @@
         for m in order:
             if mine[m]:
                 load(m, mine[m][:1], 0, True)
+                if m == order[0]:
+                    begin()
         for m in order:
             if mine[m][1:]:
                 load(m, mine[m][1:], 1, False)
@@ -217,12 +219,13 @@
     speakers = [{"c": 0}, {"xh": 0}, {"xh": 0, "c": 0}]
     barrier = pltpu.get_barrier_semaphore()
 
-    for target, is_hub in zip(targets, nearby):
-        pl.when(jnp.logical_not(is_hub))(functools.partial(greet, barrier, target))
-    pl.when(hub)(functools.partial(greet, barrier, *other_hubs))
-    pl.when(speaker)(functools.partial(greet, barrier, {"xh": 1, "c": 1}))
-    for k, norm in enumerate((norm_train, norm_step)):
-        pltpu.make_async_copy(norm, norms.at[k], small_sems.at[4]).start()
+    def begin():
+        for target, is_hub in zip(targets, nearby):
+            pl.when(jnp.logical_not(is_hub))(functools.partial(greet, barrier, target))
+        pl.when(hub)(functools.partial(greet, barrier, *other_hubs))
+        pl.when(speaker)(functools.partial(greet, barrier, {"xh": 1, "c": 1}))
+        for k, norm in enumerate((norm_train, norm_step)):
+            pltpu.make_async_copy(norm, norms.at[k], small_sems.at[4]).start()
 
     def enter(targets):
         @pl.when(hub)
@@ -309,7 +312,7 @@
         [first for first, _ in shares_of(train_gate.shape[1] // GROUP)],
         ((train_gate, low_gate, high_gate), (train_up, low_up, high_up)),
         lambda share, m, row: (outs[m], row),
-        blocks, lows, highs, load_sems, small_sems, send_sems, recv_sems, enter, between,
+        blocks, lows, highs, load_sems, small_sems, send_sems, recv_sems, begin, enter, between,
     )
 
 
@@ -320,12 +323,12 @@
 ):
     y, xl = lax.axis_index("y"), lax.axis_index("xl")
     barrier = pltpu.get_barrier_semaphore()
-    greet(barrier, {"y": lax.rem(y + 1, 4)}, {"y": lax.rem(y + 3, 4)}, {"xl": 1 - xl})
     pass_rows(
         [second for _, second in shares_of(train_gate.shape[1] // GROUP)],
         ((train_gate, low_gate, high_gate), (train_up, low_up, high_up)),
         lambda share, m, row: (out, share.index((m, row // GROUP)) * GROUP + row % GROUP),
         blocks, lows, highs, load_sems, small_sems, send_sems, recv_sems,
+        lambda: greet(barrier, {"y": lax.rem(y + 1, 4)}, {"y": lax.rem(y + 3, 4)}, {"xl": 1 - xl}),
         lambda targets: pl.semaphore_wait(barrier, len(targets)),
         lambda order: None,
     )

time: 101 us -> 101 us (level)
  no operation moved by 1% of the time
where the time goes in v9:
time: 101 us
  Pallas kernels  100 us (99%)
    pallas_call x1, Pallas kernels, per_device(): pl.pallas_call(first_kernel, out_shape=(matrix, matrix, gain), in_specs=[...  65.7 us
    pallas_call x1, Pallas kernels, per_device(): pl.pallas_call(second_kernel, out_shape=jax.ShapeDtypeStruct((most * GROU...  28.2 us
    pallas_call x1, Pallas kernels, per_device(): pl.pallas_call(write_first, out_shape=(matrix, matrix, gain), in_specs=[v...  3.65 us
    pallas_call x1, Pallas kernels, per_device(): pl.pallas_call(write_second, out_shape=(matrix, matrix), in_specs=[vmem,...  2.4 us

profile of v9, /device:TPU:0, one launch (start us, length us, event | category | flops | bytes accessed | tf_op | source)
XLA Modules:
  0.0 100.6 jit_solution(8666017082702438477)
XLA Ops:
  0.6 65.7 %shard_map.103 = (bf16[896,4096]{1,0:T(8,128)(2,1)S(1)}, bf16[896,4096]{1,0:T(8,128)(2,1)S(1)}, bf16[32,128]{1,0:T(8,128)(2,1)S(1)}) custom-call(bf16[512,896]{1,0:T(8,128)(2,1)} %train_gate.3, bf16[32,512]{1,0:T(8,128)(2,1)} %bitcast.5, bf16[32,896]{1,0:T(8,128)(2,1)} %high_gate.3, bf16[512,896]{1,0:T(8,128)(2,1)} %train_up.3, bf16[32,512]{1,0:T(8,128)(2,1)} %bitcast.7, ...), custom_call_target="tpu_custom_call" | custom-call | flops 1000000000 | bytes 20000000 | tf_op jit(solution)/shard_map/pallas_call | solution.py:403
  66.4 3.6 %shard_map.104 = (bf16[896,4096]{1,0:T(8,128)(2,1)}, bf16[896,4096]{1,0:T(8,128)(2,1)}, bf16[32,128]{1,0:T(8,128)(2,1)}) custom-call(bf16[896,4096]{1,0:T(8,128)(2,1)S(1)} %get-tuple-element.11.gate, bf16[896,4096]{1,0:T(8,128)(2,1)S(1)} %get-tuple-element.12.up, bf16[32,128]{1,0:T(8,128)(2,1)S(1)} %get-tuple-element.13.gain), custom_call_target="tpu_custom_call" | custom-call | flops 10000000 | bytes 30000000 | tf_op jit(solution)/shard_map/pallas_call | solution.py:420
  70.0 28.2 %shard_map.105.rest = bf16[640,4096]{1,0:T(8,128)(2,1)S(1)} custom-call(bf16[512,896]{1,0:T(8,128)(2,1)} %train_gate.3, bf16[32,512]{1,0:T(8,128)(2,1)} %bitcast.6, bf16[32,896]{1,0:T(8,128)(2,1)} %high_gate.3, bf16[512,896]{1,0:T(8,128)(2,1)} %train_up.3, bf16[32,512]{1,0:T(8,128)(2,1)} %bitcast.8, bf16[32,896]{1,0:T(8,128)(2,1)} %high_up.3, ...), custom_call_target="tpu_custom_call" | custom-call | flops 1000000000 | bytes 20000000 | tf_op jit(solution)/shard_map/pallas_call | solution.py:429
  98.2 2.4 %shard_map.106 = (bf16[896,4096]{1,0:T(8,128)(2,1)}, bf16[896,4096]{1,0:T(8,128)(2,1)}) custom-call(bf16[640,4096]{1,0:T(8,128)(2,1)S(1)} %shard_map.105.rest, bf16[896,4096]{1,0:T(8,128)(2,1)} %get-tuple-element.15.held_gate, bf16[896,4096]{1,0:T(8,128)(2,1)} %get-tuple-element.16.held_up), custom_call_target="tpu_custom_call", output_to_operand_aliasing={{0}: (1, {}), {1}: (2, {})} | custom-call | flops 10000000 | bytes 10000000 | tf_op jit(solution)/shard_map/pallas_call | solution.py:438
